TPU v7x, 16 devices: a whole 2x2x2 slice. The times are simulated.
16 devices in a mesh: fsdp: 16 (over z, y, x, core).
Axes of the slice: x: 2, y: 2, z: 2, core: 2. Of those that a mesh axis runs over, the one named last changes fastest.
Arguments:
- grad_mat: bfloat16 [16, 19660800], P('fsdp')
- grad_vec: bfloat16 [16, 8192], P('fsdp')
- master_mat: float32 [19660800], P('fsdp')
- moment_mat: float32 [19660800], P('fsdp')
- second_mat: float32 [19660800], P('fsdp')
- master_vec: float32 [8192], P('fsdp')
- moment_vec: float32 [8192], P('fsdp')
- second_vec: float32 [8192], P('fsdp')
Outputs:
- output 1: float32 [19660800], P('fsdp')
- output 2: float32 [19660800], P('fsdp')
- output 3: float32 [19660800], P('fsdp')
- output 4: float32 [8192], P('fsdp')
- output 5: float32 [8192], P('fsdp')
- output 6: float32 [8192], P('fsdp')
- output 7: bfloat16 [19660800], replicated
- output 8: bfloat16 [8192], replicated
All inputs are finite; a program needn't handle non-finite values.
Results may differ from a plain program's by a relative error of at most 0.001.
Values are sent between devices in bfloat16 or wider.
A program may use at most 1 GiB of HBM per device.

v0:
```python
import jax
import jax.numpy as jnp
from jax import lax
from jax.sharding import PartitionSpec as P

STEP = 4
LEARN_RATE = 1e-3
BETA_ONE = 0.9
BETA_TWO = 0.999
ADAM_EPS = 1e-8
DECAY = 0.01
NORM_EPS = 1e-6
FIX_ONE = 1.0 - BETA_ONE ** STEP
FIX_TWO = 1.0 - BETA_TWO ** STEP


def adam_update(grad_sum, clip_coef, master, moment, second, decay):
    clip_grad = clip_coef * grad_sum
    new_moment = BETA_ONE * moment + (1.0 - BETA_ONE) * clip_grad
    new_second = BETA_TWO * second + (1.0 - BETA_TWO) * clip_grad * clip_grad
    step_dir = (new_moment / FIX_ONE) / (jnp.sqrt(new_second / FIX_TWO) + ADAM_EPS)
    new_master = master - LEARN_RATE * (step_dir + decay * master)
    return new_master, new_moment, new_second


def total_share(grad_block, group):
    rows = grad_block.reshape(group, grad_block.shape[1] // group)
    received = lax.all_to_all(rows, 'fsdp', 0, 0, tiled=True)
    return jnp.sum(received, axis=0, dtype=jnp.float32)


def solution(mesh):
    group = mesh.shape['fsdp']

    def local_step(grad_mat, grad_vec, master_mat, moment_mat, second_mat, master_vec, moment_vec, second_vec):
        sum_mat = total_share(grad_mat, group)
        sum_vec = total_share(grad_vec, group)
        local_square = jnp.sum(sum_mat * sum_mat) + jnp.sum(sum_vec * sum_vec)
        total_norm = jnp.sqrt(lax.psum(local_square, 'fsdp'))
        clip_coef = jnp.minimum(1.0, 1.0 / (total_norm + NORM_EPS))
        new_mat = adam_update(sum_mat, clip_coef, master_mat, moment_mat, second_mat, DECAY)
        new_vec = adam_update(sum_vec, clip_coef, master_vec, moment_vec, second_vec, 0.0)
        weights_mat = lax.all_gather(new_mat[0].astype(jnp.bfloat16), 'fsdp', tiled=True)
        weights_vec = lax.all_gather(new_vec[0].astype(jnp.bfloat16), 'fsdp', tiled=True)
        return new_mat + new_vec + (weights_mat, weights_vec)

    row_spec = P('fsdp', None)
    flat_spec = P('fsdp')
    whole_spec = P()
    return jax.shard_map(local_step, mesh=mesh,
                         in_specs=(row_spec, row_spec) + (flat_spec,) * 6,
                         out_specs=(flat_spec,) * 6 + (whole_spec, whole_spec),
                         check_vma=False)
```

profile of v0, /device:TPU:0, one launch (start us, length us, event | category | flops | bytes accessed | tf_op | source)
XLA Modules:
  0.0 1330.0 jit_solution(16948802899490556215)
XLA Ops:
  7.2 0.5 broadcast.21
  7.7 1.5 reduce.4
  9.2 0.6 reshape.31
  9.8 5.3 all-to-all-start.1
  15.1 230.7 %reduce.3 = bf16[16,1228800]{1,0:T(8,128)(2,1)} reduce(bf16[16,1,1228800]{2,1,0:T(2,128)(2,1)} %bitcast, bf16[]{:T(256)} %broadcast.21), dimensions={1}, to_apply=%bitcast.reduce_sub_computation | reduce | bytes 78643200 | tf_op jit(solution)/shard_map/all_to_all | solution.py:28
  245.8 200.3 %reshape.29 = bf16[16,2,614400]{2,1,0:T(2,128)(2,1)} reshape(bf16[16,1228800]{1,0:T(8,128)(2,1)} %reduce.3) | data formatting | bytes 78643200
  446.1 0.0 all-to-all-done.1
  446.1 5.1 all-to-all-start
  451.1 0.0 all-gather.3.cloned.1.call-start
  451.2 0.1 convert_reduce_fusion.1
  451.3 0.6 multiply_reduce_fusion.1
  451.9 468.6 %all-to-all-done = bf16[16,2,614400]{2,1,0:T(2,128)(2,1)} async-done(((bf16[16,2,614400]{2,1,0:T(2,128)(2,1)}), bf16[16,2,614400]{2,1,0:T(2,128)(2,1)}, u32[]{:S(2)}, u32[]{:S(2)}) %all-to-all-start) | async-done | bytes 39321632 | tf_op jit(solution)/shard_map/all_to_all | solution.py:28
  920.4 95.5 %reshape.30 = bf16[16,1,1228800]{2,1,0:T(2,128)(2,1)} reshape(bf16[16,2,614400]{2,1,0:T(2,128)(2,1)} %all-to-all-done) | data formatting | bytes 78643200
  1015.9 75.7 %convert_reduce_fusion = f32[1228800]{0:T(1024)S(1)} fusion(bf16[16,1,1228800]{2,1,0:T(2,128)(2,1)} %reshape.30), kind=kLoop, calls=%fused_computation | loop fusion | flops 38092800 | bytes 44236800 | tf_op jit(solution)/shard_map/reduce_sum | solution.py:29
  1091.7 0.0 copy-start
  1091.7 2.2 copy-done
  1093.9 1.9 multiply_reduce_fusion
  1097.1 32.9 %psum.7 = f32[]{:T(128)} all-reduce(f32[]{:T(128)S(6)} %add.38), channel_id=1, replica_groups=mesh['fsdp'=16] {'fsdp'}, use_global_device_ids=true, to_apply=%region_4.0 | all-reduce | flops 1 | bytes 8 | tf_op jit(solution)/shard_map/psum | solution.py:39
  1130.7 0.0 copy-start.1
  1130.7 0.0 copy-start.2
  1130.7 0.0 copy-start.3
  1130.7 13.9 %fusion.4 = (bf16[1228800]{0:T(1024)(128)(2,1)}, f32[1228800]{0:T(1024)}, f32[1228800]{0:T(1024)}, f32[1228800]{0:T(1024)}) fusion(f32[1228800]{0:T(1024)} %param.10, f32[1228800]{0:T(1024)} %copy-done, f32[]{:T(128)S(6)} %min.3, f32[1228800]{0:T(1024)} %param.11, f32[1228800]{0:T(1024)} %param.12), kind=kLoop, calls=%fused_computation.13 | loop fusion | flops 20889600 | bytes 36864004 | tf_op jit(solution)/shard_map/convert_element_type | solution.py:43
  1144.6 0.0 all-gather.3.cloned.1.call-update
  1144.6 0.0 copy-done.1
  1144.6 0.0 copy-done.2
  1144.6 0.0 copy-done.3
  1144.6 0.6 fusion.2
  1145.3 13.6 %all-gather = bf16[16,1,512]{2,1,0:T(2,128)(2,1)S(1)} all-gather(bf16[1,1,512]{2,1,0:T(2,128)(2,1)S(1)} %reshape.26), channel_id=1, replica_groups=mesh['fsdp'=16] {'fsdp'}, dimensions={0}, use_global_device_ids=true | all-gather | bytes 17408 | tf_op jit(solution)/shard_map/all_gather | solution.py:44
  1158.9 0.1 reduce.2
  1159.0 0.6 copy.16
  1159.6 136.3 %all-gather.3.cloned.1.call-done = bf16[19660800]{0:T(1024)(128)(2,1)} async-done(((bf16[1228800]{0:T(1024)(128)(2,1)}), bf16[19660800]{0:T(1024)(128)(2,1)}) %all-gather.3.cloned.1.call-update) | async-done | bytes 39321616 | tf_op jit(solution)/shard_map/all_gather | solution.py:43
  1295.9 26.8 %copy.18 = bf16[19660800]{0:T(1024)(128)(2,1)} copy(bf16[19660800]{0:T(1024)(128)(2,1)} %all-gather.3.cloned.1.call-done) | data formatting | bytes 78643200
  (2 shorter events, 0.0 us)
Async XLA Ops:
  9.8 436.3 %all-to-all-start.1 = ((bf16[16,2,256]{2,1,0:T(2,128)(2,1)}), bf16[16,2,256]{2,1,0:T(2,128)(2,1)S(1)}, u32[]{:S(2)}, u32[]{:S(2)}) async-start(bf16[16,2,256]{2,1,0:T(2,128)(2,1)} %reshape.31), calls=%async_computation.1 | async-start | bytes 32768 | tf_op jit(solution)/shard_map/all_to_all | solution.py:28
  446.1 474.4 %all-to-all-start = ((bf16[16,2,614400]{2,1,0:T(2,128)(2,1)}), bf16[16,2,614400]{2,1,0:T(2,128)(2,1)}, u32[]{:S(2)}, u32[]{:S(2)}) async-start(bf16[16,2,614400]{2,1,0:T(2,128)(2,1)} %reshape.29), calls=%async_computation | async-start | bytes 78643200 | tf_op jit(solution)/shard_map/all_to_all | solution.py:28
  451.1 844.8 %all-gather.3.cloned.1.call-start = ((), (), s32[]{:S(2)}) async-start(), calls=%async_computation.2 | async-start | bytes 41779200 | tf_op jit(solution)/shard_map/all_gather | solution.py:43
  1091.7 2.3 copy-start
  1130.7 13.9 %copy-start.1 = (f32[512]{0:T(512)S(1)}, f32[512]{0:T(512)}, u32[]{:S(2)}) copy-start(f32[512]{0:T(512)} %param.13) | copy-start | bytes 6148
  1130.7 13.9 %copy-start.2 = (f32[512]{0:T(512)S(1)}, f32[512]{0:T(512)}, u32[]{:S(2)}) copy-start(f32[512]{0:T(512)} %param.14) | copy-start | bytes 6148
  1130.7 13.9 %copy-start.3 = (f32[512]{0:T(512)S(1)}, f32[512]{0:T(512)}, u32[]{:S(2)}) copy-start(f32[512]{0:T(512)} %param.15) | copy-start | bytes 6148
Sparse Core Ops, SparseCore 0:
  1144.7 151.1 all-gather.2
where the time goes:
time: 1340 us; the launch traced here: 1330 us
  waiting for transfers between devices  605 us (45%)
  local copies, waits for them, and re-layouts  327 us (24%)
  other arithmetic  325 us (24%)
  blocking collectives  46.5 us (3%)
  between operations  16.6 us (1%)
    all_to_all x2, waiting for transfers between devices, total_share(): received = lax.all_to_all(rows, 'fsdp', 0, 0, tiled=True)  469 us
    unnamed x15, local copies, waits for them, and re-layouts  326 us
    all_to_all x2, other arithmetic, total_share(): received = lax.all_to_all(rows, 'fsdp', 0, 0, tiled=True)  232 us
    all_gather x1, waiting for transfers between devices, local_step(): lax.all_gather(new_mat[0].astype(jnp.bfloat16), 'fsdp', tiled=True)  136 us
    reduce_sum x2, other arithmetic, total_share(): return jnp.sum(received, axis=0, dtype=jnp.float32)  75.8 us
    psum x1, blocking collectives, local_step(): total_norm = jnp.sqrt(lax.psum(local_square, 'fsdp'))  32.9 us
  transfers between devices with their start and end apart: 3, of which 2 were waited for; matrix products, arithmetic and copies ran while one was open for 33% of the time, Pallas kernels for 0%

commit v1 on v0

v1 whole, which is shorter than its diff:
```python
import functools

import jax
import jax.numpy as jnp
from jax import lax
from jax.experimental import pallas as pl
from jax.experimental.pallas import tpu as pltpu
from jax.sharding import PartitionSpec as P

STEP = 4
LEARN_RATE = 1e-3
BETA_ONE = 0.9
BETA_TWO = 0.999
ADAM_EPS = 1e-8
DECAY = 0.01
NORM_EPS = 1e-6
FIX_ONE = 1.0 - BETA_ONE ** STEP
FIX_TWO = 1.0 - BETA_TWO ** STEP

AXIS = 'fsdp'
MESH = pl.DeviceIdType.MESH
GROUP = 16
LANES = 128
ORDERS = ((2, 4, 8), (4, 8, 2), (8, 2, 4))
COLORS = len(ORDERS)
CHUNKS = 4
SUB_ROWS = 160


def adam_update(grad_sum, clip_coef, master, moment, second, decay):
    clip_grad = clip_coef * grad_sum
    new_moment = BETA_ONE * moment + (1.0 - BETA_ONE) * clip_grad
    new_second = BETA_TWO * second + (1.0 - BETA_TWO) * clip_grad * clip_grad
    step_dir = (new_moment / FIX_ONE) / (jnp.sqrt(new_second / FIX_TWO) + ADAM_EPS)
    new_master = master - LEARN_RATE * (step_dir + decay * master)
    return new_master, new_moment, new_second


def flip_of(me, bit):
    return bit * (1 - 2 * ((me // bit) % 2))


def reduce_kernel(rows, share, vec_share, grad_ref, vec_ref,
                  sum_ref, vec_sum_ref, square_ref, land_ref,
                  raw_in, raw_out, part_in, own_in, s4_out, keep0, keep1, recv2, recv3,
                  vec_land, square_land, square_acc,
                  in_sem, send1_sem, part_sem, own_sem, recv1_sem, recv2_sem, recv3_sem,
                  send2_sem, send3_sem, out_sem, small_sem):
    me = lax.axis_index(AXIS)
    core = me % 2
    block = rows * LANES
    color_len = share // COLORS
    flips = [[flip_of(me, bit) for bit in order] for order in ORDERS]

    def vec_copy(dist):
        other = (me + dist) % GROUP
        return pltpu.make_async_remote_copy(
            vec_ref.at[:, pl.ds(pl.multiple_of(other * vec_share, vec_share), vec_share)], vec_land.at[me],
            small_sem.at[0], small_sem.at[1], device_id=(other,), device_id_type=MESH)

    def vec_start(dist, carry):
        vec_copy(dist).start()
        return carry

    lax.fori_loop(1, GROUP, vec_start, 0)
    vec_own = pltpu.make_async_copy(
        vec_ref.at[:, pl.ds(pl.multiple_of(me * vec_share, vec_share), vec_share)], vec_land.at[me], small_sem.at[2])
    vec_own.start()

    def piece_at(owner, color, chunk):
        start = pl.multiple_of(owner * share + color * color_len + chunk * block, block)
        return grad_ref.at[:, pl.ds(start, block)]

    def route(item, color):
        place, kind = item // 3, (item + 1) % 3
        flip1, flip2, flip3 = flips[color]
        local = (2 - kind) // 2
        target_core = local * (1 - core) + (1 - local) * (kind - 1)
        target = me - core + (1 - local) * flip1 + target_core
        owner = target + (1 - place // 2) * flip2 + (1 - place % 2) * flip3
        source = (1 - local) * (1 + core)
        return owner, target, source, place

    def in_copy(chunk, item, color):
        owner = route(item, color)[0]
        return pltpu.make_async_copy(piece_at(owner, color, chunk), raw_in.at[item % 2, color], in_sem.at[item % 2, color])

    def pack_and_send(chunk):
        slot = chunk % 2
        for color in range(COLORS):
            in_copy(chunk, 0, color).start()

        def one_item(item, carry):
            @pl.when(item + 1 < 12)
            def _():
                for color in range(COLORS):
                    in_copy(chunk, item + 1, color).start()

            for color in range(COLORS):
                in_copy(chunk, item, color).wait()

                def pack(sub, inner):
                    off = pl.multiple_of(sub * SUB_ROWS * LANES, SUB_ROWS * LANES)
                    vals = raw_in[item % 2, color, :, pl.ds(off, SUB_ROWS * LANES)].astype(jnp.float32)
                    to = pl.multiple_of(sub * SUB_ROWS, SUB_ROWS)
                    raw_out[slot, color, item, pl.ds(to, SUB_ROWS), :] = (
                        vals.reshape(SUB_ROWS, LANES).astype(jnp.bfloat16))
                    return inner

                lax.fori_loop(0, rows // SUB_ROWS, pack, 0)
            for color in range(COLORS):
                owner, target, source, place = route(item, color)
                pltpu.make_async_remote_copy(
                    raw_out.at[slot, color, item], land_ref.at[color, chunk, place, source],
                    send1_sem.at[slot], recv1_sem.at[color, chunk], device_id=(target,), device_id_type=MESH).start()
            return carry

        lax.fori_loop(0, 12, one_item, 0)

    def wait_bytes(ref, sem):
        pltpu.make_async_copy(ref, ref, sem).wait()

    def part_copies(chunk, place, color, slot):
        flip1, flip2, flip3 = flips[color]
        owner = me + (1 - place // 2) * flip2 + (1 - place % 2) * flip3
        return (pltpu.make_async_copy(land_ref.at[color, chunk, place], part_in.at[slot, color], part_sem.at[slot, color]),
                pltpu.make_async_copy(piece_at(owner, color, chunk), own_in.at[slot, color], own_sem.at[slot, color]))

    def first_sums(chunk):
        for color in range(COLORS):
            wait_bytes(land_ref.at[color, chunk], recv1_sem.at[color, chunk])
            for copy in part_copies(chunk, 0, color, 0):
                copy.start()
        for place in range(4):
            slot = place % 2
            for color in range(COLORS):
                if place < 3:
                    for copy in part_copies(chunk, place + 1, color, (place + 1) % 2):
                        copy.start()
                for copy in part_copies(chunk, place, color, slot):
                    copy.wait()
                total = (s4_out.at[chunk, color, place] if place < 2 else
                         (keep1 if place == 2 else keep0).at[chunk, color])

                def add(sub, inner):
                    off = pl.multiple_of(sub * SUB_ROWS * LANES, SUB_ROWS * LANES)
                    to = pl.ds(pl.multiple_of(sub * SUB_ROWS, SUB_ROWS), SUB_ROWS)
                    vals = own_in[slot, color, :, pl.ds(off, SUB_ROWS * LANES)].astype(jnp.float32)
                    vals = vals.reshape(SUB_ROWS, LANES)
                    for source in range(3):
                        vals = vals + part_in[slot, color, source, to, :].astype(jnp.float32)
                    total[to, :] = vals
                    return inner

                lax.fori_loop(0, rows // SUB_ROWS, add, 0)
                if place < 2:
                    pltpu.make_async_remote_copy(
                        total, recv2.at[chunk, color, place], send2_sem, recv2_sem.at[color, chunk],
                        device_id=(me + flips[color][1],), device_id_type=MESH).start()

    pack_and_send(0)
    pack_and_send(1)

    def first_stage(chunk, carry):
        first_sums(chunk)

        @pl.when(chunk + 2 < CHUNKS)
        def _():
            wait_bytes(raw_out.at[chunk % 2], send1_sem.at[chunk % 2])
            pack_and_send(chunk + 2)

        return carry

    lax.fori_loop(0, CHUNKS, first_stage, 0)

    def second_stage(chunk, carry):
        for color in range(COLORS):
            wait_bytes(recv2.at[chunk, color], recv2_sem.at[color, chunk])

            def add(sub, inner):
                to = pl.ds(pl.multiple_of(sub * SUB_ROWS, SUB_ROWS), SUB_ROWS)
                keep1[chunk, color, to, :] += recv2[chunk, color, 0, to, :]
                keep0[chunk, color, to, :] += recv2[chunk, color, 1, to, :]
                return inner

            lax.fori_loop(0, rows // SUB_ROWS, add, 0)
            pltpu.make_async_remote_copy(
                keep1.at[chunk, color], recv3.at[chunk, color], send3_sem, recv3_sem.at[color, chunk],
                device_id=(me + flips[color][2],), device_id_type=MESH).start()
        return carry

    lax.fori_loop(0, CHUNKS, second_stage, 0)

    vec_own.wait()
    wait_bytes(vec_land.at[pl.ds(0, GROUP - 1)], small_sem.at[1])
    vec_sum = jnp.sum(vec_land[...].astype(jnp.float32), axis=0)
    vec_sum_ref[...] = vec_sum
    square_acc[...] = jnp.zeros_like(square_acc)
    vec_square = sum(vec_sum[:, part * LANES:(part + 1) * LANES] ** 2 for part in range(vec_share // LANES))

    def third_stage(chunk, carry):
        for color in range(COLORS):
            wait_bytes(recv3.at[chunk, color], recv3_sem.at[color, chunk])

            def add(sub, inner):
                to = pl.ds(pl.multiple_of(sub * SUB_ROWS, SUB_ROWS), SUB_ROWS)
                vals = keep0[chunk, color, to, :] + recv3[chunk, color, to, :]
                keep0[chunk, color, to, :] = vals
                square_acc[...] += jnp.sum((vals * vals).reshape(SUB_ROWS // 8, 8, LANES), axis=0)
                return inner

            lax.fori_loop(0, rows // SUB_ROWS, add, 0)
            start = pl.multiple_of(color * (color_len // LANES) + chunk * rows, rows)
            pltpu.make_async_copy(keep0.at[chunk, color], sum_ref.at[pl.ds(start, rows)], out_sem).start()
        return carry

    lax.fori_loop(0, CHUNKS, third_stage, 0)

    square_land[me] = jnp.sum(square_acc[...], axis=0, keepdims=True) + vec_square

    def square_copy(dist, carry):
        pltpu.make_async_remote_copy(
            square_land.at[me], square_land.at[me], small_sem.at[3], small_sem.at[4],
            device_id=((me + dist) % GROUP,), device_id_type=MESH).start()
        return carry

    lax.fori_loop(1, GROUP, square_copy, 0)
    wait_bytes(square_land.at[pl.ds(0, GROUP - 1)], small_sem.at[4])
    lane_sum = jnp.sum(square_land[...], axis=0)
    square_ref[...] = jnp.broadcast_to(jnp.sum(lane_sum, axis=1, keepdims=True), square_ref.shape)

    wait_bytes(vec_land.at[pl.ds(0, GROUP - 1)], small_sem.at[0])
    for slot in range(2):
        wait_bytes(raw_out.at[slot], send1_sem.at[slot])
    wait_bytes(s4_out, send2_sem)
    wait_bytes(keep1, send3_sem)
    wait_bytes(keep0, out_sem)
    wait_bytes(square_land.at[pl.ds(0, GROUP - 1)], small_sem.at[3])


def reduce_call(grad_mat, grad_vec):
    share = grad_mat.shape[1] // GROUP
    vec_share = grad_vec.shape[1] // GROUP
    rows = share // COLORS // CHUNKS // LANES
    any_spec = pl.BlockSpec(memory_space=pltpu.HBM)
    vmem_spec = pl.BlockSpec(memory_space=pltpu.VMEM)
    f32, bf16 = jnp.float32, jnp.bfloat16
    dma = pltpu.SemaphoreType.DMA
    return pl.pallas_call(
        functools.partial(reduce_kernel, rows, share, vec_share),
        name='reduce_share',
        out_shape=(jax.ShapeDtypeStruct((share // LANES, LANES), f32),
                   jax.ShapeDtypeStruct((1, vec_share), f32),
                   jax.ShapeDtypeStruct((1, LANES), f32),
                   jax.ShapeDtypeStruct((COLORS, CHUNKS, 4, 3, rows, LANES), bf16)),
        in_specs=[any_spec, any_spec],
        out_specs=(any_spec, vmem_spec, vmem_spec, any_spec),
        scratch_shapes=[
            pltpu.VMEM((2, COLORS, 1, rows * LANES), bf16),
            pltpu.VMEM((2, COLORS, 12, rows, LANES), bf16),
            pltpu.VMEM((2, COLORS, 3, rows, LANES), bf16),
            pltpu.VMEM((2, COLORS, 1, rows * LANES), bf16),
            pltpu.VMEM((CHUNKS, COLORS, 2, rows, LANES), f32),
            pltpu.VMEM((CHUNKS, COLORS, rows, LANES), f32),
            pltpu.VMEM((CHUNKS, COLORS, rows, LANES), f32),
            pltpu.VMEM((CHUNKS, COLORS, 2, rows, LANES), f32),
            pltpu.VMEM((CHUNKS, COLORS, rows, LANES), f32),
            pltpu.VMEM((GROUP, 1, vec_share), bf16),
            pltpu.VMEM((GROUP, 1, LANES), f32),
            pltpu.VMEM((8, LANES), f32),
            dma((2, COLORS)), dma((2,)), dma((2, COLORS)), dma((2, COLORS)),
            dma((COLORS, CHUNKS)), dma((COLORS, CHUNKS)), dma((COLORS, CHUNKS)),
            dma, dma, dma, dma((5,)),
        ],
        compiler_params=pltpu.CompilerParams(has_side_effects=True, vmem_limit_bytes=66_000_000),
    )(grad_mat, grad_vec)


def solution(mesh):
    def local_step(grad_mat, grad_vec, master_mat, moment_mat, second_mat, master_vec, moment_vec, second_vec):
        sum_mat, sum_vec, square, _ = reduce_call(grad_mat, grad_vec)
        total_norm = jnp.sqrt(square[0, 0])
        clip_coef = jnp.minimum(1.0, 1.0 / (total_norm + NORM_EPS))
        new_mat = adam_update(sum_mat.reshape(-1), clip_coef, master_mat, moment_mat, second_mat, DECAY)
        new_vec = adam_update(sum_vec.reshape(-1), clip_coef, master_vec, moment_vec, second_vec, 0.0)
        weights_mat = lax.all_gather(new_mat[0].astype(jnp.bfloat16), AXIS, tiled=True)
        weights_vec = lax.all_gather(new_vec[0].astype(jnp.bfloat16), AXIS, tiled=True)
        return new_mat + new_vec + (weights_mat, weights_vec)

    row_spec = P(AXIS, None)
    flat_spec = P(AXIS)
    whole_spec = P()
    return jax.shard_map(local_step, mesh=mesh,
                         in_specs=(row_spec, row_spec) + (flat_spec,) * 6,
                         out_specs=(flat_spec,) * 6 + (whole_spec, whole_spec),
                         check_vma=False)
```

time: 1340 us -> 467 us (0.35)
  waiting for transfers between devices: 605 us -> 136 us
  other arithmetic: 325 us -> 14.4 us
  local copies, waits for them, and re-layouts: 327 us -> 27.4 us
  Pallas kernels: 0 us -> 261 us
  blocking collectives: 46.5 us -> 11.8 us
    all_to_all x2 -> x0, waiting for transfers between devices: 469 us -> none  [total_share(): received = lax.all_to_all(rows, 'fsdp', 0, 0, tiled=True)]
    unnamed x15 -> x11, local copies, waits for them, and re-layouts: 326 us -> 27.4 us
    pallas_call x0 -> x1, Pallas kernels: none -> 261 us  [reduce_call(): pl.pallas_call(functools.partial(reduce_kernel, rows, share, vec_share),...]
    all_to_all x2 -> x0, other arithmetic: 232 us -> none  [total_share(): received = lax.all_to_all(rows, 'fsdp', 0, 0, tiled=True)]
    reduce_sum x4 -> x0, other arithmetic: 78.2 us -> none  [the longest x2 75.8 us: total_share(): return jnp.sum(received, axis=0, dtype=jnp.float32)]
    psum x1 -> x0, blocking collectives: 32.9 us -> none  [local_step(): total_norm = jnp.sqrt(lax.psum(local_square, 'fsdp'))]
  transfers between devices with their start and end apart: 3 -> 1, of which waited for: 2 -> 1; matrix products, arithmetic and copies ran while one was open for 33% -> 0% of each run, Pallas kernels for 0% -> 0%
where the time goes in v1:
time: 467 us; the launch traced here: 466 us
  Pallas kernels  261 us (56%)
  waiting for transfers between devices  136 us (29%)
  local copies, waits for them, and re-layouts  27.4 us (6%)
  between operations  14.9 us (3%)
  other arithmetic  14.4 us (3%)
  blocking collectives  11.8 us (3%)
    pallas_call x1, Pallas kernels, reduce_call(): pl.pallas_call(functools.partial(reduce_kernel, rows, share, vec_share),...  261 us
    all_gather x1, waiting for transfers between devices, local_step(): lax.all_gather(new_mat[0].astype(jnp.bfloat16), AXIS, tiled=True)  136 us
    unnamed x11, local copies, waits for them, and re-layouts  27.4 us
    convert_element_type x1, other arithmetic, local_step(): new_mat[0].astype(jnp.bfloat16)  13.7 us
    all_gather x1, blocking collectives, local_step(): lax.all_gather(new_vec[0].astype(jnp.bfloat16), AXIS, tiled=True)  11.8 us
  transfers between devices with their start and end apart: 1, of which 1 were waited for; matrix products, arithmetic and copies ran while one was open for 0% of the time, Pallas kernels for 0%

profile of v1, /device:TPU:0, one launch (start us, length us, event | category | flops | bytes accessed | tf_op | source)
XLA Modules:
  0.0 466.0 jit_solution(14037638582758920753)
XLA Ops:
  7.2 0.0 all-gather.3.cloned.1.call-start
  7.2 261.0 %reduce_share.1 = (f32[9600,128]{1,0:T(8,128)}, f32[1,512]{1,0:T(1,128)}, f32[1,128]{1,0:T(1,128)}, bf16[3,4,4,3,800,128]{5,4,3,2,1,0:T(8,128)(2,1)}) custom-call(bf16[1,19660800]{1,0:T(2,128)(2,1)} %grad_ref.1, bf16[1,8192]{1,0:T(2,128)(2,1)} %vec_ref.1), custom_call_target="tpu_custom_call" | custom-call | tf_op jit(solution)/shard_map/reduce_share/pallas_call | solution.py:249
  269.0 0.0 copy-start.3
  269.0 0.0 copy-start
  269.0 0.0 copy-start.1
  269.1 0.0 copy-start.2
  269.1 13.7 %fusion.5 = (bf16[1228800]{0:T(1024)(128)(2,1)}, f32[1228800]{0:T(1024)}, f32[1228800]{0:T(1024)}, f32[1228800]{0:T(1024)}) fusion(f32[1228800]{0:T(1024)} %param.10, f32[9600,128]{1,0:T(8,128)} %get-tuple-element.12, f32[]{:T(128)} %bitcast, f32[1228800]{0:T(1024)} %param.11, f32[1228800]{0:T(1024)} %param.12), kind=kLoop, calls=%fused_computation.11 | loop fusion | flops 20889600 | bytes 36864004 | tf_op jit(solution)/shard_map/convert_element_type | solution.py:286
  282.8 0.0 all-gather.3.cloned.1.call-update
  282.8 0.0 copy-done.3
  282.8 0.0 copy-done
  282.8 0.0 copy-done.1
  282.8 0.0 copy-done.2
  282.9 0.6 fusion.3
  283.5 11.8 %all-gather = bf16[16,1,512]{2,1,0:T(2,128)(2,1)S(1)} all-gather(bf16[1,1,512]{2,1,0:T(2,128)(2,1)S(1)} %reshape.29), channel_id=1, replica_groups=mesh['fsdp'=16] {'fsdp'}, dimensions={0}, use_global_device_ids=true | all-gather | bytes 17408 | tf_op jit(solution)/shard_map/all_gather | solution.py:287
  295.2 0.1 reduce
  295.3 0.6 copy.16
  295.9 136.5 %all-gather.3.cloned.1.call-done = bf16[19660800]{0:T(1024)(128)(2,1)} async-done(((bf16[1228800]{0:T(1024)(128)(2,1)}), bf16[19660800]{0:T(1024)(128)(2,1)}) %all-gather.3.cloned.1.call-update) | async-done | bytes 39321616 | tf_op jit(solution)/shard_map/all_gather | solution.py:286
  432.4 26.8 %copy.18 = bf16[19660800]{0:T(1024)(128)(2,1)} copy(bf16[19660800]{0:T(1024)(128)(2,1)} %all-gather.3.cloned.1.call-done) | data formatting | bytes 78643200
  (2 shorter events, 0.0 us)
Async XLA Ops:
  7.2 425.3 %all-gather.3.cloned.1.call-start = ((), (), s32[]{:S(2)}) async-start(), calls=%async_computation | async-start | bytes 41779200 | tf_op jit(solution)/shard_map/all_gather | solution.py:286
  269.0 13.8 %copy-start.3 = (f32[1,512]{1,0:T(1,128)S(1)}, f32[1,512]{1,0:T(1,128)}, u32[]{:S(2)}) copy-start(f32[1,512]{1,0:T(1,128)} %get-tuple-element.13) | copy-start | bytes 6148
  269.0 13.8 %copy-start = (f32[512]{0:T(512)S(1)}, f32[512]{0:T(512)}, u32[]{:S(2)}) copy-start(f32[512]{0:T(512)} %param.13) | copy-start | bytes 6148
  269.0 13.8 %copy-start.1 = (f32[512]{0:T(512)S(1)}, f32[512]{0:T(512)}, u32[]{:S(2)}) copy-start(f32[512]{0:T(512)} %param.14) | copy-start | bytes 6148
  269.1 13.8 %copy-start.2 = (f32[512]{0:T(512)S(1)}, f32[512]{0:T(512)}, u32[]{:S(2)}) copy-start(f32[512]{0:T(512)} %param.15) | copy-start | bytes 6148
Sparse Core Ops, SparseCore 0:
  282.9 149.4 all-gather.2

commit v2 on v1

--- a/solution.py
+++ b/solution.py
@@ -25,6 +25,9 @@
 COLORS = len(ORDERS)
 CHUNKS = 4
 SUB_ROWS = 160
+UPDATE_ROWS = 80
+GATHER_VMEM = 8_000_000
+STORE_VMEM = GATHER_VMEM
 
 
 def adam_update(grad_sum, clip_coef, master, moment, second, decay):
@@ -276,16 +279,201 @@
     )(grad_mat, grad_vec)
 
 
+def gather_kernel(rows, share, vec_share, sum_ref, vec_sum_ref, square_ref, master_ref, moment_ref, second_ref,
+                  vec_master_ref, vec_moment_ref, vec_second_ref,
+                  new_master_ref, new_moment_ref, new_second_ref,
+                  vec_new_master_ref, vec_new_moment_ref, vec_new_second_ref, land_ref, vec_land_ref,
+                  state_in, state_sem, send_sem, recv_sem, core_send_sem, core_recv_sem, vec_sem):
+    me = lax.axis_index(AXIS)
+    partner = me + flip_of(me, 1)
+    flips = [[flip_of(me, bit) for bit in order] for order in ORDERS]
+    color_rows = share // COLORS // LANES
+
+    def rows_at(color, chunk):
+        return pl.ds(pl.multiple_of(color * color_rows + chunk * rows, rows), rows)
+
+    def state_copies(chunk, color, slot):
+        at = rows_at(color, chunk)
+        return [pltpu.make_async_copy(ref.at[at], state_in.at[slot, index], state_sem.at[slot, index])
+                for index, ref in enumerate((sum_ref, master_ref, moment_ref, second_ref))]
+
+    def link_copy(stage, owner, color, chunk, hop):
+        piece = land_ref.at[owner, rows_at(color, chunk)]
+        return pltpu.make_async_remote_copy(
+            piece, piece, send_sem.at[color], recv_sem.at[stage, color, chunk],
+            device_id=(me + flips[color][hop],), device_id_type=MESH)
+
+    def core_copy(owner, color, chunk):
+        piece = land_ref.at[owner, rows_at(color, chunk)]
+        return pltpu.make_async_remote_copy(
+            piece, piece, core_send_sem.at[color], core_recv_sem.at[color],
+            device_id=(partner,), device_id_type=MESH)
+
+    for copy in state_copies(0, 0, 0):
+        copy.start()
+    norm = jnp.sqrt(square_ref[...][:, :1])
+    clip_coef = jnp.minimum(1.0, 1.0 / (norm + NORM_EPS))
+
+    def update_chunk(chunk, carry):
+        for color in range(COLORS):
+            item = chunk * COLORS + color
+            slot = item % 2
+            if color + 1 < COLORS:
+                for copy in state_copies(chunk, color + 1, (item + 1) % 2):
+                    copy.start()
+            else:
+                @pl.when(chunk + 1 < CHUNKS)
+                def _():
+                    for copy in state_copies(chunk + 1, 0, (item + 1) % 2):
+                        copy.start()
+            for copy in state_copies(chunk, color, slot):
+                copy.wait()
+            base = color * color_rows + chunk * rows
+
+            def update(sub, inner):
+                to = pl.ds(pl.multiple_of(sub * UPDATE_ROWS, UPDATE_ROWS), UPDATE_ROWS)
+                out = pl.ds(pl.multiple_of(base + sub * UPDATE_ROWS, UPDATE_ROWS), UPDATE_ROWS)
+                master, moment, second = adam_update(
+                    state_in[slot, 0, to, :], clip_coef, state_in[slot, 1, to, :],
+                    state_in[slot, 2, to, :], state_in[slot, 3, to, :], DECAY)
+                new_master_ref[out, :] = master
+                new_moment_ref[out, :] = moment
+                new_second_ref[out, :] = second
+                land_ref[me, out, :] = master.astype(jnp.bfloat16)
+                return inner
+
+            lax.fori_loop(0, rows // UPDATE_ROWS, update, 0)
+            link_copy(0, me, color, chunk, 0).start()
+        return carry
+
+    lax.fori_loop(0, CHUNKS, update_chunk, 0)
+
+    vec_new = adam_update(vec_sum_ref[...], clip_coef, vec_master_ref[...], vec_moment_ref[...], vec_second_ref[...], 0.0)
+    vec_new_master_ref[...], vec_new_moment_ref[...], vec_new_second_ref[...] = vec_new
+    vec_land_ref[me] = vec_new[0].reshape(vec_share // LANES, LANES)
+
+    def own_sends(chunk, carry):
+        for color in range(COLORS):
+            link_copy(1, me, color, chunk, 1).start()
+            core_copy(me, color, chunk).start()
+        return carry
+
+    lax.fori_loop(0, CHUNKS, own_sends, 0)
+
+    def own_sends_last(chunk, carry):
+        for color in range(COLORS):
+            link_copy(3, me, color, chunk, 2).start()
+        return carry
+
+    lax.fori_loop(0, CHUNKS, own_sends_last, 0)
+
+    def vec_send(dist, carry):
+        pltpu.make_async_remote_copy(
+            vec_land_ref.at[me], vec_land_ref.at[me], vec_sem.at[0], vec_sem.at[1],
+            device_id=((me + dist) % GROUP,), device_id_type=MESH).start()
+        return carry
+
+    lax.fori_loop(1, GROUP, vec_send, 0)
+
+    def arrivals(stage, hops, onward):
+        def one_chunk(chunk, carry):
+            for color in range(COLORS):
+                owner = me + sum(flips[color][hop] for hop in hops)
+                pltpu.make_async_copy(land_ref.at[owner, rows_at(color, chunk)], land_ref.at[owner, rows_at(color, chunk)],
+                                      recv_sem.at[stage, color, chunk]).wait()
+                for next_stage, hop in onward:
+                    link_copy(next_stage, owner, color, chunk, hop).start()
+                core_copy(owner, color, chunk).start()
+            return carry
+
+        lax.fori_loop(0, CHUNKS, one_chunk, 0)
+
+    arrivals(0, (0,), ((2, 1), (4, 2)))
+    arrivals(1, (1,), ((5, 2),))
+    arrivals(3, (2,), ())
+    arrivals(2, (0, 1), ((6, 2),))
+    arrivals(4, (0, 2), ())
+    arrivals(5, (1, 2), ())
+    arrivals(6, (0, 1, 2), ())
+
+    def wait_bytes(ref, sem):
+        pltpu.make_async_copy(ref, ref, sem).wait()
+
+    for color in range(COLORS):
+        eight = land_ref.at[pl.ds(0, 8), pl.ds(color * color_rows, color_rows)]
+        wait_bytes(land_ref.at[pl.ds(0, 7), pl.ds(color * color_rows, color_rows)], send_sem.at[color])
+        wait_bytes(eight, core_send_sem.at[color])
+        wait_bytes(eight, core_recv_sem.at[color])
+    for index in range(2):
+        wait_bytes(vec_land_ref.at[pl.ds(0, GROUP - 1)], vec_sem.at[index])
+
+
+def gather_call(sums, states, vec_states):
+    sum_mat, sum_vec, square = sums
+    share, vec_share = sum_mat.size, sum_vec.size
+    rows = share // COLORS // CHUNKS // LANES
+    hbm_spec = pl.BlockSpec(memory_space=pltpu.HBM)
+    vmem_spec = pl.BlockSpec(memory_space=pltpu.VMEM)
+    f32, bf16 = jnp.float32, jnp.bfloat16
+    dma = pltpu.SemaphoreType.DMA
+    mat_out = pltpu.VMEM((share // LANES, LANES), f32)
+    vec_out = pltpu.VMEM((1, vec_share), f32)
+    return pl.pallas_call(
+        functools.partial(gather_kernel, rows, share, vec_share),
+        name='update_gather',
+        out_shape=(mat_out,) * 3 + (vec_out,) * 3 + (
+            pltpu.VMEM((GROUP, share // LANES, LANES), bf16), pltpu.VMEM((GROUP, vec_share // LANES, LANES), f32)),
+        in_specs=[hbm_spec, vmem_spec, vmem_spec] + [hbm_spec] * 3 + [vmem_spec] * 3,
+        out_specs=(vmem_spec,) * 8,
+        scratch_shapes=[
+            pltpu.VMEM((2, 4, rows, LANES), f32), dma((2, 4)),
+            dma((COLORS,)), dma((7, COLORS, CHUNKS)), dma((COLORS,)), dma((COLORS,)), dma((2,)),
+        ],
+        compiler_params=pltpu.CompilerParams(has_side_effects=True, vmem_limit_bytes=GATHER_VMEM),
+    )(sum_mat, sum_vec, square, *states, *vec_states)
+
+
+def store_kernel(*refs):
+    ins, outs, (vec_weights, sems) = refs[:8], refs[8:16], refs[16:]
+    land, vec_land = ins[6:]
+    copies = [pltpu.make_async_copy(source, target, sems.at[index])
+              for index, (source, target) in enumerate(zip(ins[:6], outs[:6]))]
+    for owner in range(GROUP):
+        copies.append(pltpu.make_async_copy(land.at[owner], outs[6].at[owner], sems.at[6 + owner]))
+    for copy in copies:
+        copy.start()
+    vec_rows = vec_land.shape[1]
+    for owner in range(GROUP):
+        vec_weights[owner * vec_rows:(owner + 1) * vec_rows, :] = vec_land[owner]
+    outs[7][...] = vec_weights[...].astype(jnp.bfloat16)
+    for copy in copies:
+        copy.wait()
+
+
+def store_call(results):
+    vmem_spec = pl.BlockSpec(memory_space=pltpu.VMEM)
+    hbm_spec = pl.BlockSpec(memory_space=pltpu.HBM)
+    dma = pltpu.SemaphoreType.DMA
+    vec_rows = results[7].size // LANES
+    return pl.pallas_call(
+        store_kernel,
+        name='store_results',
+        out_shape=tuple(jax.ShapeDtypeStruct(result.shape, result.dtype) for result in results[:7]) + (
+            jax.ShapeDtypeStruct((vec_rows, LANES), jnp.bfloat16),),
+        in_specs=[vmem_spec] * 8,
+        out_specs=(hbm_spec,) * 7 + (vmem_spec,),
+        scratch_shapes=[pltpu.VMEM((vec_rows, LANES), jnp.float32), dma((6 + GROUP,))],
+        compiler_params=pltpu.CompilerParams(vmem_limit_bytes=STORE_VMEM),
+    )(*[pltpu.with_memory_space_constraint(result, pltpu.VMEM) for result in results])
+
+
 def solution(mesh):
     def local_step(grad_mat, grad_vec, master_mat, moment_mat, second_mat, master_vec, moment_vec, second_vec):
-        sum_mat, sum_vec, square, _ = reduce_call(grad_mat, grad_vec)
-        total_norm = jnp.sqrt(square[0, 0])
-        clip_coef = jnp.minimum(1.0, 1.0 / (total_norm + NORM_EPS))
-        new_mat = adam_update(sum_mat.reshape(-1), clip_coef, master_mat, moment_mat, second_mat, DECAY)
-        new_vec = adam_update(sum_vec.reshape(-1), clip_coef, master_vec, moment_vec, second_vec, 0.0)
-        weights_mat = lax.all_gather(new_mat[0].astype(jnp.bfloat16), AXIS, tiled=True)
-        weights_vec = lax.all_gather(new_vec[0].astype(jnp.bfloat16), AXIS, tiled=True)
-        return new_mat + new_vec + (weights_mat, weights_vec)
+        sums = reduce_call(grad_mat, grad_vec)[:3]
+        states = [state.reshape(-1, LANES) for state in (master_mat, moment_mat, second_mat)]
+        vec_states = [state.reshape(1, -1) for state in (master_vec, moment_vec, second_vec)]
+        results = store_call(gather_call(sums, states, vec_states))
+        return tuple(result.reshape(-1) for result in results)
 
     row_spec = P(AXIS, None)
     flat_spec = P(AXIS)

time: 467 us -> 417 us (0.89)
  Pallas kernels: 261 us -> 415 us
  waiting for transfers between devices: 136 us -> 0 us
  local copies, waits for them, and re-layouts: 27.4 us -> 0 us
  other arithmetic: 14.4 us -> 0 us
  between operations: 14.9 us -> 0.65 us
  blocking collectives: 11.8 us -> 0 us
    pallas_call x0 -> x2, Pallas kernels: none -> 154 us  [the longest x1 136 us: gather_call(): pl.pallas_call(functools.partial(gather_kernel, rows, share, vec_share),...]
    all_gather x1 -> x0, waiting for transfers between devices: 136 us -> none  [local_step(): lax.all_gather(new_mat[0].astype(jnp.bfloat16), AXIS, tiled=True)]
    unnamed x11 -> x0, local copies, waits for them, and re-layouts: 27.4 us -> none
    convert_element_type x2 -> x0, other arithmetic: 14.3 us -> none  [the longest x1 13.7 us: local_step(): new_mat[0].astype(jnp.bfloat16)]
    all_gather x1 -> x0, blocking collectives: 11.8 us -> none  [local_step(): lax.all_gather(new_vec[0].astype(jnp.bfloat16), AXIS, tiled=True)]
  transfers between devices with their start and end apart: 1 -> 0, of which waited for: 1 -> 0; matrix products, arithmetic and copies ran while one was open for 0% -> 0% of each run, Pallas kernels for 0% -> 0%
where the time goes in v2:
time: 417 us; the launch traced here: 416 us
  Pallas kernels  415 us (100%)
    pallas_call x1, Pallas kernels, reduce_call(): pl.pallas_call(functools.partial(reduce_kernel, rows, share, vec_share),...  261 us
    pallas_call x1, Pallas kernels, gather_call(): pl.pallas_call(functools.partial(gather_kernel, rows, share, vec_share),...  136 us
    pallas_call x1, Pallas kernels, store_call(): pl.pallas_call(store_kernel, name='store_results', out_shape=tuple((jax.S...  17.9 us

profile of v2, /device:TPU:0, one launch (start us, length us, event | category | flops | bytes accessed | tf_op | source)
XLA Modules:
  0.0 415.7 jit_solution(409367798161668674)
XLA Ops:
  0.6 261.0 %reduce_share.1 = (f32[9600,128]{1,0:T(8,128)}, f32[1,512]{1,0:T(1,128)}, f32[1,128]{1,0:T(1,128)}, bf16[3,4,4,3,800,128]{5,4,3,2,1,0:T(8,128)(2,1)}) custom-call(bf16[1,19660800]{1,0:T(2,128)(2,1)} %grad_ref.1, bf16[1,8192]{1,0:T(2,128)(2,1)} %vec_ref.1), custom_call_target="tpu_custom_call" | custom-call | tf_op jit(solution)/shard_map/reduce_share/pallas_call | solution.py:252
  261.7 136.1 %update_gather.1 = (f32[9600,128]{1,0:T(8,128)S(1)}, f32[9600,128]{1,0:T(8,128)S(1)}, f32[9600,128]{1,0:T(8,128)S(1)}, f32[1,512]{1,0:T(1,128)S(1)}, f32[1,512]{...) custom-call(f32[9600,128]{1,0:T(8,128)} %get-tuple-element.27.sum_ref, ...), custom_call_target="tpu_custom_call" | custom-call | tf_op jit(solution)/shard_map/update_gather/pallas_call | solution.py:421
  397.8 17.9 %store_results.1 = (f32[9600,128]{1,0:T(8,128)}, f32[9600,128]{1,0:T(8,128)}, f32[9600,128]{1,0:T(8,128)}, f32[1,512]{1,0:T(1,128)}, f32[1,512]{1,0:T(1,128)}, /...) custom-call(f32[9600,128]{1,0:T(8,128)S(1)} %get-tuple-element.30.refs_0_, ...), custom_call_target="tpu_custom_call" | custom-call | tf_op jit(solution)/shard_map/store_results/pallas_call | solution.py:458

commit v3 on v2

v3 whole, which is shorter than its diff:
```python
import functools

import jax
import jax.numpy as jnp
from jax import lax
from jax.experimental import pallas as pl
from jax.experimental.pallas import tpu as pltpu
from jax.sharding import PartitionSpec as P

STEP = 4
LEARN_RATE = 1e-3
BETA_ONE = 0.9
BETA_TWO = 0.999
ADAM_EPS = 1e-8
DECAY = 0.01
NORM_EPS = 1e-6
FIX_ONE = 1.0 - BETA_ONE ** STEP
FIX_TWO = 1.0 - BETA_TWO ** STEP

AXIS = 'fsdp'
MESH = pl.DeviceIdType.MESH
GROUP = 16
LANES = 128
ORDERS = ((2, 4, 8), (4, 8, 2), (8, 2, 4))
COLORS = len(ORDERS)
CHUNKS = 8
AHEAD = 3
SUB_ROWS = 80
UPDATE_ROWS = 80
RING = 4
ITEMS = 12
SCRATCH_BYTES = 12_700_000


def adam_update(grad_sum, clip_coef, master, moment, second, decay):
    clip_grad = clip_coef * grad_sum
    new_moment = BETA_ONE * moment + (1.0 - BETA_ONE) * clip_grad
    new_second = BETA_TWO * second + (1.0 - BETA_TWO) * clip_grad * clip_grad
    step_dir = (new_moment / FIX_ONE) / (jnp.sqrt(new_second / FIX_TWO) + ADAM_EPS)
    new_master = master - LEARN_RATE * (step_dir + decay * master)
    return new_master, new_moment, new_second


def flip_of(me, bit):
    return bit * (1 - 2 * ((me // bit) % 2))


def step_kernel(rows, share, vec_share, grad_ref, vec_ref, master_ref, moment_ref, second_ref,
                vec_master_ref, vec_moment_ref, vec_second_ref,
                new_master_ref, new_moment_ref, new_second_ref,
                vec_new_master_ref, vec_new_moment_ref, vec_new_second_ref, weights_ref, vec_weights_ref,
                land_ref, recv2,
                pad_in, keep, recv2_in, recv3, vec_land, square_land, square_acc,
                pad_sem, part_sem, recv2_in_sem, state_sem,
                send1_sem, send2_sem, send3_sem, recv1_sem, recv2_sem, recv3_sem, small_sem,
                send_sem, recv_sem, core_send_sem, core_recv_sem):
    me = lax.axis_index(AXIS)
    core = me % 2
    partner = me + flip_of(me, 1)
    block = rows * LANES
    color_len = share // COLORS
    color_rows = color_len // LANES
    flips = [[flip_of(me, bit) for bit in order] for order in ORDERS]
    per_owner = share // LANES // rows

    def wait_bytes(ref, sem):
        pltpu.make_async_copy(ref, ref, sem).wait()

    def rows_at(color, chunk):
        return pl.ds(pl.multiple_of(color * color_rows + chunk * rows, rows), rows)

    def piece_at(owner, color, chunk):
        start = pl.multiple_of(owner * share + color * color_len + chunk * block, block)
        return grad_ref.at[:, pl.ds(start, block)]

    def packed_at(index):
        return index // per_owner, pl.multiple_of((index % per_owner) * rows, rows)

    def packed_index(color, chunk, item):
        return (chunk * COLORS + color) * ITEMS + item

    part_owner = COLORS * CHUNKS * ITEMS // per_owner
    part_rows = 3 * rows

    def part_at(slot, color):
        return (slot * COLORS + color) * part_rows

    def small_copy(dist):
        other = (me + dist) % GROUP
        return pltpu.make_async_remote_copy(
            vec_ref.at[:, pl.ds(pl.multiple_of(other * vec_share, vec_share), vec_share)], vec_land.at[me],
            small_sem.at[0], small_sem.at[1], device_id=(other,), device_id_type=MESH)

    def small_start(dist, carry):
        small_copy(dist).start()
        return carry

    def route(item, color):
        place, kind = item // 3, (item + 1) % 3
        flip1, flip2, flip3 = flips[color]
        local = (2 - kind) // 2
        target_core = local * (1 - core) + (1 - local) * (kind - 1)
        target = me - core + (1 - local) * flip1 + target_core
        owner = target + (1 - place // 2) * flip2 + (1 - place % 2) * flip3
        source = (1 - local) * (1 + core)
        return owner, target, source, place

    def in_copy(chunk, item, color):
        owner = route(item, color)[0]
        return pltpu.make_async_copy(piece_at(owner, color, chunk), pad_in.at[item % 2, color], pad_sem.at[item % 2, color])

    def pack_and_send(chunk):
        for color in range(COLORS):
            in_copy(chunk, 0, color).start()

        def one_item(item, carry):
            @pl.when(item + 1 < ITEMS)
            def _():
                for color in range(COLORS):
                    in_copy(chunk, item + 1, color).start()

            for color in range(COLORS):
                in_copy(chunk, item, color).wait()
                place_owner, place_row = packed_at(packed_index(color, chunk, item))

                def pack(sub, inner):
                    off = pl.multiple_of(sub * SUB_ROWS * LANES, SUB_ROWS * LANES)
                    vals = pad_in[item % 2, color, :, pl.ds(off, SUB_ROWS * LANES)].astype(jnp.float32)
                    to = pl.multiple_of(place_row + sub * SUB_ROWS, SUB_ROWS)
                    weights_ref[place_owner, pl.ds(to, SUB_ROWS), :] = (
                        vals.reshape(SUB_ROWS, LANES).astype(jnp.bfloat16))
                    return inner

                lax.fori_loop(0, rows // SUB_ROWS, pack, 0, unroll=True)
            for color in range(COLORS):
                owner, target, source, place = route(item, color)
                place_owner, place_row = packed_at(packed_index(color, chunk, item))
                pltpu.make_async_remote_copy(
                    weights_ref.at[place_owner, pl.ds(place_row, rows)],
                    land_ref.at[color, chunk, place, pl.ds(pl.multiple_of(source * rows, rows), rows)],
                    send1_sem.at[chunk], recv1_sem.at[color, chunk], device_id=(target,), device_id_type=MESH).start()
            return carry

        lax.fori_loop(0, ITEMS, one_item, 0)

    def part_copies(chunk, place, color, slot):
        flip1, flip2, flip3 = flips[color]
        owner = me + (1 - place // 2) * flip2 + (1 - place % 2) * flip3
        return (pltpu.make_async_copy(land_ref.at[color, chunk, place],
                                      weights_ref.at[part_owner, pl.ds(part_at(slot, color), part_rows)],
                                      part_sem.at[slot, color]),
                pltpu.make_async_copy(piece_at(owner, color, chunk), pad_in.at[slot, color], pad_sem.at[slot, color]))

    def first_sums(chunk):
        for color in range(COLORS):
            wait_bytes(land_ref.at[color, chunk], recv1_sem.at[color, chunk])
            for copy in part_copies(chunk, 0, color, 0):
                copy.start()
        for place in range(4):
            slot = place % 2
            for color in range(COLORS):
                if place < 3:
                    for copy in part_copies(chunk, place + 1, color, (place + 1) % 2):
                        copy.start()
                for copy in part_copies(chunk, place, color, slot):
                    copy.wait()
                at = rows_at(color, chunk)
                total = (new_moment_ref.at[at], new_second_ref.at[at], keep.at[chunk, color], new_master_ref.at[at])[place]

                def add(sub, inner):
                    off = pl.multiple_of(sub * SUB_ROWS * LANES, SUB_ROWS * LANES)
                    to = pl.ds(pl.multiple_of(sub * SUB_ROWS, SUB_ROWS), SUB_ROWS)
                    vals = pad_in[slot, color, :, pl.ds(off, SUB_ROWS * LANES)].astype(jnp.float32)
                    vals = vals.reshape(SUB_ROWS, LANES)
                    for source in range(3):
                        row = pl.multiple_of(part_at(slot, color) + source * rows + sub * SUB_ROWS, SUB_ROWS)
                        vals = vals + weights_ref[part_owner, pl.ds(row, SUB_ROWS), :].astype(jnp.float32)
                    total[to, :] = vals
                    return inner

                lax.fori_loop(0, rows // SUB_ROWS, add, 0, unroll=True)
                if place < 2:
                    pltpu.make_async_remote_copy(
                        total, recv2.at[chunk, color, place], send2_sem.at[place], recv2_sem.at[color, chunk],
                        device_id=(me + flips[color][1],), device_id_type=MESH).start()

    pack_and_send(0)
    lax.fori_loop(1, GROUP, small_start, 0)
    vec_own = pltpu.make_async_copy(
        vec_ref.at[:, pl.ds(pl.multiple_of(me * vec_share, vec_share), vec_share)], vec_land.at[me], small_sem.at[2])
    vec_own.start()

    def pack_ahead(chunk, carry):
        pack_and_send(chunk)
        return carry

    lax.fori_loop(1, AHEAD, pack_ahead, 0)

    def first_stage(chunk, carry):
        first_sums(chunk)

        @pl.when(chunk + AHEAD < CHUNKS)
        def _():
            pack_and_send(chunk + AHEAD)

        return carry

    lax.fori_loop(0, CHUNKS, first_stage, 0)

    def second_stage(chunk, carry):
        copies = [pltpu.make_async_copy(recv2.at[chunk, color], recv2_in.at[color], recv2_in_sem.at[color])
                  for color in range(COLORS)]
        for color in range(COLORS):
            wait_bytes(recv2.at[chunk, color], recv2_sem.at[color, chunk])
            copies[color].start()
        for color in range(COLORS):
            copies[color].wait()
            base = color * color_rows + chunk * rows

            def add(sub, inner):
                to = pl.ds(pl.multiple_of(sub * SUB_ROWS, SUB_ROWS), SUB_ROWS)
                out = pl.ds(pl.multiple_of(base + sub * SUB_ROWS, SUB_ROWS), SUB_ROWS)
                keep[chunk, color, to, :] += recv2_in[color, 0, to, :]
                new_master_ref[out, :] += recv2_in[color, 1, to, :]
                return inner

            lax.fori_loop(0, rows // SUB_ROWS, add, 0)
            pltpu.make_async_remote_copy(
                keep.at[chunk, color], recv3.at[chunk, color], send3_sem.at[chunk], recv3_sem.at[color, chunk],
                device_id=(me + flips[color][2],), device_id_type=MESH).start()
        return carry

    lax.fori_loop(0, CHUNKS, second_stage, 0)

    vec_own.wait()
    wait_bytes(vec_land.at[pl.ds(0, GROUP - 1)], small_sem.at[1])
    vec_sum = jnp.sum(vec_land[...].astype(jnp.float32), axis=0)
    square_acc[...] = jnp.zeros_like(square_acc)
    vec_square = sum(vec_sum[:, part * LANES:(part + 1) * LANES] ** 2 for part in range(vec_share // LANES))

    def third_stage(chunk, carry):
        for color in range(COLORS):
            wait_bytes(recv3.at[chunk, color], recv3_sem.at[color, chunk])
            base = color * color_rows + chunk * rows

            def add(sub, inner):
                to = pl.ds(pl.multiple_of(sub * SUB_ROWS, SUB_ROWS), SUB_ROWS)
                out = pl.ds(pl.multiple_of(base + sub * SUB_ROWS, SUB_ROWS), SUB_ROWS)
                vals = new_master_ref[out, :] + recv3[chunk, color, to, :]
                new_master_ref[out, :] = vals
                square_acc[...] += jnp.sum((vals * vals).reshape(SUB_ROWS // 8, 8, LANES), axis=0)
                return inner

            lax.fori_loop(0, rows // SUB_ROWS, add, 0)
        return carry

    def state_copies(chunk, color):
        slot = (chunk * COLORS + color) % RING
        at = rows_at(color, chunk)
        return [pltpu.make_async_copy(ref.at[at], keep.at[slot, index], state_sem.at[slot, index])
                for index, ref in enumerate((master_ref, moment_ref, second_ref))]

    lax.fori_loop(0, CHUNKS - 2, third_stage, 0)
    for chunk in range(RING):
        wait_bytes(keep.at[chunk], send3_sem.at[chunk])
    for item in range(RING):
        for copy in state_copies(item // COLORS, item % COLORS):
            copy.start()
    lax.fori_loop(CHUNKS - 2, CHUNKS, third_stage, 0)

    def wait_packed(chunk, carry):
        wait_bytes(weights_ref.at[pl.ds(0, COLORS), pl.ds(0, ITEMS * rows)], send1_sem.at[chunk])
        return carry

    lax.fori_loop(0, CHUNKS, wait_packed, 0)
    square_land[me] = jnp.sum(square_acc[...], axis=0, keepdims=True) + vec_square

    def square_copy(dist, carry):
        pltpu.make_async_remote_copy(
            square_land.at[me], square_land.at[me], small_sem.at[3], small_sem.at[4],
            device_id=((me + dist) % GROUP,), device_id_type=MESH).start()
        return carry

    lax.fori_loop(1, GROUP, square_copy, 0)
    wait_bytes(new_moment_ref, send2_sem.at[0])
    wait_bytes(new_second_ref, send2_sem.at[1])
    wait_bytes(square_land.at[pl.ds(0, GROUP - 1)], small_sem.at[4])
    norm = jnp.sqrt(jnp.sum(jnp.sum(square_land[...], axis=0), axis=1, keepdims=True))
    clip_coef = jnp.minimum(1.0, 1.0 / (norm + NORM_EPS))

    def link_copy(stage, owner, color, chunk, hop):
        piece = weights_ref.at[owner, rows_at(color, chunk)]
        return pltpu.make_async_remote_copy(
            piece, piece, send_sem.at[color], recv_sem.at[stage, color, chunk],
            device_id=(me + flips[color][hop],), device_id_type=MESH)

    def core_copy(owner, color, chunk):
        piece = weights_ref.at[owner, rows_at(color, chunk)]
        return pltpu.make_async_remote_copy(
            piece, piece, core_send_sem.at[color], core_recv_sem.at[color],
            device_id=(partner,), device_id_type=MESH)

    def update_chunk(chunk, carry):
        for color in range(COLORS):
            item = chunk * COLORS + color
            slot = item % RING
            for copy in state_copies(chunk, color):
                copy.wait()
            base = color * color_rows + chunk * rows

            def update(sub, inner):
                to = pl.ds(pl.multiple_of(sub * UPDATE_ROWS, UPDATE_ROWS), UPDATE_ROWS)
                out = pl.ds(pl.multiple_of(base + sub * UPDATE_ROWS, UPDATE_ROWS), UPDATE_ROWS)
                master, moment, second = adam_update(
                    new_master_ref[out, :], clip_coef, keep[slot, 0, to, :],
                    keep[slot, 1, to, :], keep[slot, 2, to, :], DECAY)
                new_master_ref[out, :] = master
                new_moment_ref[out, :] = moment
                new_second_ref[out, :] = second
                weights_ref[me, out, :] = master.astype(jnp.bfloat16)
                return inner

            lax.fori_loop(0, rows // UPDATE_ROWS, update, 0)
            link_copy(0, me, color, chunk, 0).start()

            @pl.when(item + RING < CHUNKS * COLORS)
            def _():
                for copy in state_copies((item + RING) // COLORS, (item + RING) % COLORS):
                    copy.start()
        return carry

    lax.fori_loop(0, CHUNKS, update_chunk, 0)

    vec_new = adam_update(vec_sum, clip_coef, vec_master_ref[...], vec_moment_ref[...], vec_second_ref[...], 0.0)
    vec_new_master_ref[...], vec_new_moment_ref[...], vec_new_second_ref[...] = vec_new
    vec_weights_ref[me] = vec_new[0].reshape(vec_share // LANES, LANES)

    def own_sends(chunk, carry):
        for color in range(COLORS):
            link_copy(1, me, color, chunk, 1).start()
            core_copy(me, color, chunk).start()
        return carry

    lax.fori_loop(0, CHUNKS, own_sends, 0)

    def own_sends_last(chunk, carry):
        for color in range(COLORS):
            link_copy(3, me, color, chunk, 2).start()
        return carry

    lax.fori_loop(0, CHUNKS, own_sends_last, 0)

    def vec_send(dist, carry):
        pltpu.make_async_remote_copy(
            vec_weights_ref.at[me], vec_weights_ref.at[me], small_sem.at[5], small_sem.at[6],
            device_id=((me + dist) % GROUP,), device_id_type=MESH).start()
        return carry

    lax.fori_loop(1, GROUP, vec_send, 0)

    def arrivals(stage, hops, onward):
        def one_chunk(chunk, carry):
            for color in range(COLORS):
                owner = me + sum(flips[color][hop] for hop in hops)
                wait_bytes(weights_ref.at[owner, rows_at(color, chunk)], recv_sem.at[stage, color, chunk])
                for next_stage, hop in onward:
                    link_copy(next_stage, owner, color, chunk, hop).start()
                core_copy(owner, color, chunk).start()
            return carry

        lax.fori_loop(0, CHUNKS, one_chunk, 0)

    arrivals(0, (0,), ((2, 1), (4, 2)))
    arrivals(1, (1,), ((5, 2),))
    arrivals(3, (2,), ())
    arrivals(2, (0, 1), ((6, 2),))
    arrivals(4, (0, 2), ())
    arrivals(5, (1, 2), ())
    arrivals(6, (0, 1, 2), ())

    for color in range(COLORS):
        eight = weights_ref.at[pl.ds(0, 8), pl.ds(color * color_rows, color_rows)]
        wait_bytes(weights_ref.at[pl.ds(0, 7), pl.ds(color * color_rows, color_rows)], send_sem.at[color])
        wait_bytes(eight, core_send_sem.at[color])
        wait_bytes(eight, core_recv_sem.at[color])
    for index in (5, 6):
        wait_bytes(vec_weights_ref.at[pl.ds(0, GROUP - 1)], small_sem.at[index])
    for chunk in range(RING, CHUNKS):
        wait_bytes(keep.at[chunk], send3_sem.at[chunk])
    wait_bytes(vec_land.at[pl.ds(0, GROUP - 1)], small_sem.at[0])
    wait_bytes(square_land.at[pl.ds(0, GROUP - 1)], small_sem.at[3])


def step_call(grad_mat, grad_vec, states, vec_states):
    share = grad_mat.shape[1] // GROUP
    vec_share = grad_vec.shape[1] // GROUP
    rows = share // COLORS // CHUNKS // LANES
    hbm_spec = pl.BlockSpec(memory_space=pltpu.HBM)
    vmem_spec = pl.BlockSpec(memory_space=pltpu.VMEM)
    f32, bf16 = jnp.float32, jnp.bfloat16
    dma = pltpu.SemaphoreType.DMA
    return pl.pallas_call(
        functools.partial(step_kernel, rows, share, vec_share),
        name='adam_step',
        out_shape=(pltpu.VMEM((share // LANES, LANES), f32),) * 3 + (pltpu.VMEM((1, vec_share), f32),) * 3 + (
            pltpu.VMEM((GROUP, share // LANES, LANES), bf16),
            pltpu.VMEM((GROUP, vec_share // LANES, LANES), f32),
            jax.ShapeDtypeStruct((COLORS, CHUNKS, 4, 3 * rows, LANES), bf16),
            jax.ShapeDtypeStruct((CHUNKS, COLORS, 2, rows, LANES), f32)),
        in_specs=[hbm_spec] * 5 + [vmem_spec] * 3,
        out_specs=(vmem_spec,) * 8 + (hbm_spec,) * 2,
        scratch_shapes=[
            pltpu.VMEM((2, COLORS, 1, rows * LANES), bf16),
            pltpu.VMEM((CHUNKS, COLORS, rows, LANES), f32),
            pltpu.VMEM((COLORS, 2, rows, LANES), f32),
            pltpu.VMEM((CHUNKS, COLORS, rows, LANES), f32),
            pltpu.VMEM((GROUP, 1, vec_share), bf16),
            pltpu.VMEM((GROUP, 1, LANES), f32),
            pltpu.VMEM((8, LANES), f32),
            dma((2, COLORS)), dma((2, COLORS)), dma((COLORS,)), dma((RING, 3)),
            dma((CHUNKS,)), dma((2,)), dma((CHUNKS,)),
            dma((COLORS, CHUNKS)), dma((COLORS, CHUNKS)), dma((COLORS, CHUNKS)), dma((7,)),
            dma((COLORS,)), dma((7, COLORS, CHUNKS)), dma((COLORS,)), dma((COLORS,)),
        ],
        compiler_params=pltpu.CompilerParams(has_side_effects=True, vmem_limit_bytes=SCRATCH_BYTES),
    )(grad_mat, grad_vec, *states, *vec_states)[:8]


def store_kernel(*refs):
    ins, outs, (vec_weights, sems) = refs[:8], refs[8:16], refs[16:]
    land, vec_land = ins[6:]
    copies = [pltpu.make_async_copy(source, target, sems.at[index])
              for index, (source, target) in enumerate(zip(ins[:6], outs[:6]))]
    for owner in range(GROUP):
        copies.append(pltpu.make_async_copy(land.at[owner], outs[6].at[owner], sems.at[6 + owner]))
    for copy in copies:
        copy.start()
    vec_rows = vec_land.shape[1]
    for owner in range(GROUP):
        vec_weights[owner * vec_rows:(owner + 1) * vec_rows, :] = vec_land[owner]
    outs[7][...] = vec_weights[...].astype(jnp.bfloat16)
    for copy in copies:
        copy.wait()


def store_call(results):
    vmem_spec = pl.BlockSpec(memory_space=pltpu.VMEM)
    hbm_spec = pl.BlockSpec(memory_space=pltpu.HBM)
    dma = pltpu.SemaphoreType.DMA
    vec_rows = results[7].size // LANES
    return pl.pallas_call(
        store_kernel,
        name='store_results',
        out_shape=tuple(jax.ShapeDtypeStruct(result.shape, result.dtype) for result in results[:7]) + (
            jax.ShapeDtypeStruct((vec_rows, LANES), jnp.bfloat16),),
        in_specs=[vmem_spec] * 8,
        out_specs=(hbm_spec,) * 7 + (vmem_spec,),
        scratch_shapes=[pltpu.VMEM((vec_rows, LANES), jnp.float32), dma((6 + GROUP,))],
        compiler_params=pltpu.CompilerParams(vmem_limit_bytes=SCRATCH_BYTES),
    )(*[pltpu.with_memory_space_constraint(result, pltpu.VMEM) for result in results])


def solution(mesh):
    def local_step(grad_mat, grad_vec, master_mat, moment_mat, second_mat, master_vec, moment_vec, second_vec):
        states = [state.reshape(-1, LANES) for state in (master_mat, moment_mat, second_mat)]
        vec_states = [state.reshape(1, -1) for state in (master_vec, moment_vec, second_vec)]
        results = store_call(step_call(grad_mat, grad_vec, states, vec_states))
        return tuple(result.reshape(-1) for result in results)

    row_spec = P(AXIS, None)
    flat_spec = P(AXIS)
    whole_spec = P()
    return jax.shard_map(local_step, mesh=mesh,
                         in_specs=(row_spec, row_spec) + (flat_spec,) * 6,
                         out_specs=(flat_spec,) * 6 + (whole_spec, whole_spec),
                         check_vma=False)
```

time: 417 us -> 412 us (0.988)
  Pallas kernels: 415 us -> 409 us
    pallas_call x2 -> x1, Pallas kernels: 397 us -> 391 us  [step_call(): pl.pallas_call(functools.partial(step_kernel, rows, share, vec_share), na...]
where the time goes in v3:
time: 412 us; the launch traced here: 409 us
  Pallas kernels  409 us (99%)
    pallas_call x1, Pallas kernels, step_call(): pl.pallas_call(functools.partial(step_kernel, rows, share, vec_share), na...  391 us
    pallas_call x1, Pallas kernels, store_call(): pl.pallas_call(store_kernel, name='store_results', out_shape=tuple((jax.S...  17.9 us

profile of v3, /device:TPU:0, one launch (start us, length us, event | category | flops | bytes accessed | tf_op | source)
XLA Modules:
  0.0 409.2 jit_solution(15341834023811278972)
XLA Ops:
  0.6 390.7 %adam_step.1 = (f32[9600,128]{1,0:T(8,128)S(1)}, f32[9600,128]{1,0:T(8,128)S(1)}, f32[9600,128]{1,0:T(8,128)S(1)}, f32[1,512]{1,0:T(1,128)S(1)}, f32[1,512]{1,0:...) custom-call(bf16[1,19660800]{1,0:T(2,128)(2,1)} %grad_ref.1, ...), custom_call_target="tpu_custom_call" | custom-call | tf_op jit(solution)/shard_map/adam_step/pallas_call | solution.py:402
  391.3 17.9 %store_results.1 = (f32[9600,128]{1,0:T(8,128)}, f32[9600,128]{1,0:T(8,128)}, f32[9600,128]{1,0:T(8,128)}, f32[1,512]{1,0:T(1,128)}, f32[1,512]{1,0:T(1,128)}, /...) custom-call(f32[9600,128]{1,0:T(8,128)S(1)} %get-tuple-element.24.refs_0_, ...), custom_call_target="tpu_custom_call" | custom-call | tf_op jit(solution)/shard_map/store_results/pallas_call | solution.py:451

commit v4 on v3

--- a/solution.py
+++ b/solution.py
@@ -28,6 +28,7 @@
 SUB_ROWS = 80
 UPDATE_ROWS = 80
 RING = 4
+STATE_PARTS = 2
 ITEMS = 12
 SCRATCH_BYTES = 12_700_000
 
@@ -62,6 +63,9 @@
     color_rows = color_len // LANES
     flips = [[flip_of(me, bit) for bit in order] for order in ORDERS]
     per_owner = share // LANES // rows
+    neighbours = [partner] + [me + flip_of(me, bit) + other for bit in ORDERS[0] for other in (0, flip_of(me, 1))]
+    others = [me + sum(flip_of(me, bit) for bit in (1, 2, 4, 8) if mask & bit)
+              for mask in sorted(range(1, GROUP), key=lambda mask: (-(mask >> 1).bit_count(), mask))]
 
     def wait_bytes(ref, sem):
         pltpu.make_async_copy(ref, ref, sem).wait()
@@ -84,16 +88,6 @@
 
     def part_at(slot, color):
         return (slot * COLORS + color) * part_rows
-
-    def small_copy(dist):
-        other = (me + dist) % GROUP
-        return pltpu.make_async_remote_copy(
-            vec_ref.at[:, pl.ds(pl.multiple_of(other * vec_share, vec_share), vec_share)], vec_land.at[me],
-            small_sem.at[0], small_sem.at[1], device_id=(other,), device_id_type=MESH)
-
-    def small_start(dist, carry):
-        small_copy(dist).start()
-        return carry
 
     def route(item, color):
         place, kind = item // 3, (item + 1) % 3
@@ -109,39 +103,45 @@
         owner = route(item, color)[0]
         return pltpu.make_async_copy(piece_at(owner, color, chunk), pad_in.at[item % 2, color], pad_sem.at[item % 2, color])
 
-    def pack_and_send(chunk):
-        for color in range(COLORS):
-            in_copy(chunk, 0, color).start()
-
+    def start_in(chunk, item):
+        for color in range(COLORS):
+            in_copy(chunk, item, color).start()
+
+    def pack_item(chunk, item):
+        for color in range(COLORS):
+            in_copy(chunk, item, color).wait()
+            place_owner, place_row = packed_at(packed_index(color, chunk, item))
+
+            def pack(sub, inner):
+                off = pl.multiple_of(sub * SUB_ROWS * LANES, SUB_ROWS * LANES)
+                vals = pad_in[item % 2, color, :, pl.ds(off, SUB_ROWS * LANES)].astype(jnp.float32)
+                to = pl.multiple_of(place_row + sub * SUB_ROWS, SUB_ROWS)
+                weights_ref[place_owner, pl.ds(to, SUB_ROWS), :] = (
+                    vals.reshape(SUB_ROWS, LANES).astype(jnp.bfloat16))
+                return inner
+
+            lax.fori_loop(0, rows // SUB_ROWS, pack, 0, unroll=True)
+
+    def send_item(chunk, item):
+        for color in range(COLORS):
+            owner, target, source, place = route(item, color)
+            place_owner, place_row = packed_at(packed_index(color, chunk, item))
+            pltpu.make_async_remote_copy(
+                weights_ref.at[place_owner, pl.ds(place_row, rows)],
+                land_ref.at[color, chunk, place, pl.ds(pl.multiple_of(source * rows, rows), rows)],
+                send1_sem.at[chunk], recv1_sem.at[color, chunk], device_id=(target,), device_id_type=MESH).start()
+
+    def pack_and_send(chunk, first):
         def one_item(item, carry):
             @pl.when(item + 1 < ITEMS)
             def _():
-                for color in range(COLORS):
-                    in_copy(chunk, item + 1, color).start()
-
-            for color in range(COLORS):
-                in_copy(chunk, item, color).wait()
-                place_owner, place_row = packed_at(packed_index(color, chunk, item))
-
-                def pack(sub, inner):
-                    off = pl.multiple_of(sub * SUB_ROWS * LANES, SUB_ROWS * LANES)
-                    vals = pad_in[item % 2, color, :, pl.ds(off, SUB_ROWS * LANES)].astype(jnp.float32)
-                    to = pl.multiple_of(place_row + sub * SUB_ROWS, SUB_ROWS)
-                    weights_ref[place_owner, pl.ds(to, SUB_ROWS), :] = (
-                        vals.reshape(SUB_ROWS, LANES).astype(jnp.bfloat16))
-                    return inner
-
-                lax.fori_loop(0, rows // SUB_ROWS, pack, 0, unroll=True)
-            for color in range(COLORS):
-                owner, target, source, place = route(item, color)
-                place_owner, place_row = packed_at(packed_index(color, chunk, item))
-                pltpu.make_async_remote_copy(
-                    weights_ref.at[place_owner, pl.ds(place_row, rows)],
-                    land_ref.at[color, chunk, place, pl.ds(pl.multiple_of(source * rows, rows), rows)],
-                    send1_sem.at[chunk], recv1_sem.at[color, chunk], device_id=(target,), device_id_type=MESH).start()
+                start_in(chunk, item + 1)
+
+            pack_item(chunk, item)
+            send_item(chunk, item)
             return carry
 
-        lax.fori_loop(0, ITEMS, one_item, 0)
+        lax.fori_loop(first, ITEMS, one_item, 0)
 
     def part_copies(chunk, place, color, slot):
         flip1, flip2, flip3 = flips[color]
@@ -184,14 +184,19 @@
                         total, recv2.at[chunk, color, place], send2_sem.at[place], recv2_sem.at[color, chunk],
                         device_id=(me + flips[color][1],), device_id_type=MESH).start()
 
-    pack_and_send(0)
-    lax.fori_loop(1, GROUP, small_start, 0)
-    vec_own = pltpu.make_async_copy(
-        vec_ref.at[:, pl.ds(pl.multiple_of(me * vec_share, vec_share), vec_share)], vec_land.at[me], small_sem.at[2])
-    vec_own.start()
+    start_in(0, 0)
+    start_in(0, 1)
+    barrier = pltpu.get_barrier_semaphore()
+    for neighbour in neighbours:
+        pl.semaphore_signal(barrier, inc=1, device_id=(neighbour,), device_id_type=MESH)
+    pack_item(0, 0)
+    pl.semaphore_wait(barrier, len(neighbours))
+    send_item(0, 0)
+    pack_and_send(0, 1)
 
     def pack_ahead(chunk, carry):
-        pack_and_send(chunk)
+        start_in(chunk, 0)
+        pack_and_send(chunk, 0)
         return carry
 
     lax.fori_loop(1, AHEAD, pack_ahead, 0)
@@ -201,7 +206,8 @@
 
         @pl.when(chunk + AHEAD < CHUNKS)
         def _():
-            pack_and_send(chunk + AHEAD)
+            start_in(chunk + AHEAD, 0)
+            pack_and_send(chunk + AHEAD, 0)
 
         return carry
 
@@ -230,13 +236,17 @@
                 device_id=(me + flips[color][2],), device_id_type=MESH).start()
         return carry
 
-    lax.fori_loop(0, CHUNKS, second_stage, 0)
-
-    vec_own.wait()
-    wait_bytes(vec_land.at[pl.ds(0, GROUP - 1)], small_sem.at[1])
-    vec_sum = jnp.sum(vec_land[...].astype(jnp.float32), axis=0)
+    second_stage(0, 0)
+    for other in others:
+        pltpu.make_async_remote_copy(
+            vec_ref.at[:, pl.ds(pl.multiple_of(other * vec_share, vec_share), vec_share)], vec_land.at[me],
+            small_sem.at[0], small_sem.at[1], device_id=(other,), device_id_type=MESH).start()
+    vec_own = pltpu.make_async_copy(
+        vec_ref.at[:, pl.ds(pl.multiple_of(me * vec_share, vec_share), vec_share)], vec_land.at[me], small_sem.at[2])
+    vec_own.start()
+    lax.fori_loop(1, CHUNKS, second_stage, 0)
+
     square_acc[...] = jnp.zeros_like(square_acc)
-    vec_square = sum(vec_sum[:, part * LANES:(part + 1) * LANES] ** 2 for part in range(vec_share // LANES))
 
     def third_stage(chunk, carry):
         for color in range(COLORS):
@@ -266,22 +276,25 @@
     for item in range(RING):
         for copy in state_copies(item // COLORS, item % COLORS):
             copy.start()
-    lax.fori_loop(CHUNKS - 2, CHUNKS, third_stage, 0)
+    third_stage(CHUNKS - 2, 0)
+
+    vec_own.wait()
+    wait_bytes(vec_land.at[pl.ds(0, GROUP - 1)], small_sem.at[1])
+    vec_sum = jnp.sum(vec_land[...].astype(jnp.float32), axis=0)
+    vec_square = sum(vec_sum[:, part * LANES:(part + 1) * LANES] ** 2 for part in range(vec_share // LANES))
 
     def wait_packed(chunk, carry):
         wait_bytes(weights_ref.at[pl.ds(0, COLORS), pl.ds(0, ITEMS * rows)], send1_sem.at[chunk])
         return carry
 
     lax.fori_loop(0, CHUNKS, wait_packed, 0)
+    third_stage(CHUNKS - 1, 0)
     square_land[me] = jnp.sum(square_acc[...], axis=0, keepdims=True) + vec_square
 
-    def square_copy(dist, carry):
+    for other in others:
         pltpu.make_async_remote_copy(
             square_land.at[me], square_land.at[me], small_sem.at[3], small_sem.at[4],
-            device_id=((me + dist) % GROUP,), device_id_type=MESH).start()
-        return carry
-
-    lax.fori_loop(1, GROUP, square_copy, 0)
+            device_id=(other,), device_id_type=MESH).start()
     wait_bytes(new_moment_ref, send2_sem.at[0])
     wait_bytes(new_second_ref, send2_sem.at[1])
     wait_bytes(square_land.at[pl.ds(0, GROUP - 1)], small_sem.at[4])
@@ -323,6 +336,11 @@
             lax.fori_loop(0, rows // UPDATE_ROWS, update, 0)
             link_copy(0, me, color, chunk, 0).start()
 
+            @pl.when(chunk == 0)
+            def _():
+                link_copy(1, me, color, chunk, 1).start()
+                link_copy(3, me, color, chunk, 2).start()
+
             @pl.when(item + RING < CHUNKS * COLORS)
             def _():
                 for copy in state_copies((item + RING) // COLORS, (item + RING) % COLORS):
@@ -337,7 +355,10 @@
 
     def own_sends(chunk, carry):
         for color in range(COLORS):
-            link_copy(1, me, color, chunk, 1).start()
+            @pl.when(chunk > 0)
+            def _():
+                link_copy(1, me, color, chunk, 1).start()
+
             core_copy(me, color, chunk).start()
         return carry
 
@@ -348,15 +369,12 @@
             link_copy(3, me, color, chunk, 2).start()
         return carry
 
-    lax.fori_loop(0, CHUNKS, own_sends_last, 0)
-
-    def vec_send(dist, carry):
+    lax.fori_loop(1, CHUNKS, own_sends_last, 0)
+
+    for other in others:
         pltpu.make_async_remote_copy(
             vec_weights_ref.at[me], vec_weights_ref.at[me], small_sem.at[5], small_sem.at[6],
-            device_id=((me + dist) % GROUP,), device_id_type=MESH).start()
-        return carry
-
-    lax.fori_loop(1, GROUP, vec_send, 0)
+            device_id=(other,), device_id_type=MESH).start()
 
     def arrivals(stage, hops, onward):
         def one_chunk(chunk, carry):
@@ -422,17 +440,21 @@
             dma((COLORS, CHUNKS)), dma((COLORS, CHUNKS)), dma((COLORS, CHUNKS)), dma((7,)),
             dma((COLORS,)), dma((7, COLORS, CHUNKS)), dma((COLORS,)), dma((COLORS,)),
         ],
-        compiler_params=pltpu.CompilerParams(has_side_effects=True, vmem_limit_bytes=SCRATCH_BYTES),
+        compiler_params=pltpu.CompilerParams(
+            collective_id=0, has_side_effects=True, vmem_limit_bytes=SCRATCH_BYTES),
     )(grad_mat, grad_vec, *states, *vec_states)[:8]
 
 
 def store_kernel(*refs):
     ins, outs, (vec_weights, sems) = refs[:8], refs[8:16], refs[16:]
     land, vec_land = ins[6:]
-    copies = [pltpu.make_async_copy(source, target, sems.at[index])
-              for index, (source, target) in enumerate(zip(ins[:6], outs[:6]))]
+    places = [(ins[index], outs[index]) for index in range(3, 6)]
+    for index in range(3):
+        part = ins[index].shape[0] // STATE_PARTS
+        places += [(ins[index].at[pl.ds(at * part, part)], outs[index].at[pl.ds(at * part, part)]) for at in range(STATE_PARTS)]
     for owner in range(GROUP):
-        copies.append(pltpu.make_async_copy(land.at[owner], outs[6].at[owner], sems.at[6 + owner]))
+        places.append((land.at[owner], outs[6].at[owner]))
+    copies = [pltpu.make_async_copy(source, target, sems.at[index]) for index, (source, target) in enumerate(places)]
     for copy in copies:
         copy.start()
     vec_rows = vec_land.shape[1]
@@ -455,7 +477,7 @@
             jax.ShapeDtypeStruct((vec_rows, LANES), jnp.bfloat16),),
         in_specs=[vmem_spec] * 8,
         out_specs=(hbm_spec,) * 7 + (vmem_spec,),
-        scratch_shapes=[pltpu.VMEM((vec_rows, LANES), jnp.float32), dma((6 + GROUP,))],
+        scratch_shapes=[pltpu.VMEM((vec_rows, LANES), jnp.float32), dma((3 + 3 * STATE_PARTS + GROUP,))],
         compiler_params=pltpu.CompilerParams(vmem_limit_bytes=SCRATCH_BYTES),
     )(*[pltpu.with_memory_space_constraint(result, pltpu.VMEM) for result in results])
 

time: 412 us -> 407 us (0.988)
  Pallas kernels: 409 us -> 404 us
    pallas_call x1, Pallas kernels: 391 us -> 386 us  [step_call(): pl.pallas_call(functools.partial(step_kernel, rows, share, vec_share), na...]
where the time goes in v4:
time: 407 us; the launch traced here: 405 us
  Pallas kernels  404 us (99%)
    pallas_call x1, Pallas kernels, step_call(): pl.pallas_call(functools.partial(step_kernel, rows, share, vec_share), na...  386 us
    pallas_call x1, Pallas kernels, store_call(): pl.pallas_call(store_kernel, name='store_results', out_shape=tuple((jax.S...  17.9 us

profile of v4, /device:TPU:0, one launch (start us, length us, event | category | flops | bytes accessed | tf_op | source)
XLA Modules:
  0.0 404.6 jit_solution(988723536334118000)
XLA Ops:
  0.6 386.0 %adam_step.1 = (f32[9600,128]{1,0:T(8,128)S(1)}, f32[9600,128]{1,0:T(8,128)S(1)}, f32[9600,128]{1,0:T(8,128)S(1)}, f32[1,512]{1,0:T(1,128)S(1)}, f32[1,512]{1,0:...) custom-call(bf16[1,19660800]{1,0:T(2,128)(2,1)} %grad_ref.1, ...), custom_call_target="tpu_custom_call" | custom-call | tf_op jit(solution)/shard_map/adam_step/pallas_call | solution.py:420
  386.7 17.9 %store_results.1 = (f32[9600,128]{1,0:T(8,128)}, f32[9600,128]{1,0:T(8,128)}, f32[9600,128]{1,0:T(8,128)}, f32[1,512]{1,0:T(1,128)}, f32[1,512]{1,0:T(1,128)}, /...) custom-call(f32[9600,128]{1,0:T(8,128)S(1)} %get-tuple-element.24.refs_0_, ...), custom_call_target="tpu_custom_call" | custom-call | tf_op jit(solution)/shard_map/store_results/pallas_call | solution.py:473

commit v5 on v4

--- a/solution.py
+++ b/solution.py
@@ -253,15 +253,15 @@
             wait_bytes(recv3.at[chunk, color], recv3_sem.at[color, chunk])
             base = color * color_rows + chunk * rows
 
-            def add(sub, inner):
+            def add(sub, squares):
                 to = pl.ds(pl.multiple_of(sub * SUB_ROWS, SUB_ROWS), SUB_ROWS)
                 out = pl.ds(pl.multiple_of(base + sub * SUB_ROWS, SUB_ROWS), SUB_ROWS)
                 vals = new_master_ref[out, :] + recv3[chunk, color, to, :]
                 new_master_ref[out, :] = vals
-                square_acc[...] += jnp.sum((vals * vals).reshape(SUB_ROWS // 8, 8, LANES), axis=0)
-                return inner
-
-            lax.fori_loop(0, rows // SUB_ROWS, add, 0)
+                return squares + jnp.sum((vals * vals).reshape(SUB_ROWS // 8, 8, LANES), axis=0)
+
+            squares = lax.fori_loop(0, rows // SUB_ROWS, add, jnp.zeros((8, LANES), jnp.float32), unroll=True)
+            square_acc[...] += squares
         return carry
 
     def state_copies(chunk, color):
@@ -301,8 +301,8 @@
     norm = jnp.sqrt(jnp.sum(jnp.sum(square_land[...], axis=0), axis=1, keepdims=True))
     clip_coef = jnp.minimum(1.0, 1.0 / (norm + NORM_EPS))
 
-    def link_copy(stage, owner, color, chunk, hop):
-        piece = weights_ref.at[owner, rows_at(color, chunk)]
+    def link_copy(stage, owner, color, chunk, hop, part=None):
+        piece = weights_ref.at[owner, rows_at(color, chunk) if part is None else part]
         return pltpu.make_async_remote_copy(
             piece, piece, send_sem.at[color], recv_sem.at[stage, color, chunk],
             device_id=(me + flips[color][hop],), device_id_type=MESH)
@@ -313,7 +313,7 @@
             piece, piece, core_send_sem.at[color], core_recv_sem.at[color],
             device_id=(partner,), device_id_type=MESH)
 
-    def update_chunk(chunk, carry):
+    def update_chunk(chunk, first):
         for color in range(COLORS):
             item = chunk * COLORS + color
             slot = item % RING
@@ -331,23 +331,26 @@
                 new_moment_ref[out, :] = moment
                 new_second_ref[out, :] = second
                 weights_ref[me, out, :] = master.astype(jnp.bfloat16)
+                if first:
+                    for stage, hop in ((0, 0), (1, 1), (3, 2)):
+                        link_copy(stage, me, color, chunk, hop, out).start()
                 return inner
 
             lax.fori_loop(0, rows // UPDATE_ROWS, update, 0)
-            link_copy(0, me, color, chunk, 0).start()
-
-            @pl.when(chunk == 0)
-            def _():
-                link_copy(1, me, color, chunk, 1).start()
-                link_copy(3, me, color, chunk, 2).start()
+            if not first:
+                link_copy(0, me, color, chunk, 0).start()
 
             @pl.when(item + RING < CHUNKS * COLORS)
             def _():
                 for copy in state_copies((item + RING) // COLORS, (item + RING) % COLORS):
                     copy.start()
-        return carry
-
-    lax.fori_loop(0, CHUNKS, update_chunk, 0)
+
+    def update_later(chunk, carry):
+        update_chunk(chunk, False)
+        return carry
+
+    update_chunk(0, True)
+    lax.fori_loop(1, CHUNKS, update_later, 0)
 
     vec_new = adam_update(vec_sum, clip_coef, vec_master_ref[...], vec_moment_ref[...], vec_second_ref[...], 0.0)
     vec_new_master_ref[...], vec_new_moment_ref[...], vec_new_second_ref[...] = vec_new

time: 407 us -> 407 us (level)
  no operation moved by 1% of the time
where the time goes in v5:
time: 407 us; the launch traced here: 404 us
  Pallas kernels  404 us (99%)
    pallas_call x1, Pallas kernels, step_call(): pl.pallas_call(functools.partial(step_kernel, rows, share, vec_share), na...  386 us
    pallas_call x1, Pallas kernels, store_call(): pl.pallas_call(store_kernel, name='store_results', out_shape=tuple((jax.S...  17.9 us

profile of v5, /device:TPU:0, one launch (start us, length us, event | category | flops | bytes accessed | tf_op | source)
XLA Modules:
  0.0 404.2 jit_solution(7999858734779976259)
XLA Ops:
  0.6 385.6 %adam_step.1 = (f32[9600,128]{1,0:T(8,128)S(1)}, f32[9600,128]{1,0:T(8,128)S(1)}, f32[9600,128]{1,0:T(8,128)S(1)}, f32[1,512]{1,0:T(1,128)S(1)}, f32[1,512]{1,0:...) custom-call(bf16[1,19660800]{1,0:T(2,128)(2,1)} %grad_ref.1, ...), custom_call_target="tpu_custom_call" | custom-call | tf_op jit(solution)/shard_map/adam_step/pallas_call | solution.py:423
  386.3 17.9 %store_results.1 = (f32[9600,128]{1,0:T(8,128)}, f32[9600,128]{1,0:T(8,128)}, f32[9600,128]{1,0:T(8,128)}, f32[1,512]{1,0:T(1,128)}, f32[1,512]{1,0:T(1,128)}, /...) custom-call(f32[9600,128]{1,0:T(8,128)S(1)} %get-tuple-element.24.refs_0_, ...), custom_call_target="tpu_custom_call" | custom-call | tf_op jit(solution)/shard_map/store_results/pallas_call | solution.py:476

commit v6 on v5

--- a/solution.py
+++ b/solution.py
@@ -25,12 +25,13 @@
 COLORS = len(ORDERS)
 CHUNKS = 8
 AHEAD = 3
+SLOTS = 3
 SUB_ROWS = 80
 UPDATE_ROWS = 80
 RING = 4
 STATE_PARTS = 2
 ITEMS = 12
-SCRATCH_BYTES = 12_700_000
+SCRATCH_BYTES = 12_800_000
 
 
 def adam_update(grad_sum, clip_coef, master, moment, second, decay):
@@ -86,9 +87,6 @@
     part_owner = COLORS * CHUNKS * ITEMS // per_owner
     part_rows = 3 * rows
 
-    def part_at(slot, color):
-        return (slot * COLORS + color) * part_rows
-
     def route(item, color):
         place, kind = item // 3, (item + 1) % 3
         flip1, flip2, flip3 = flips[color]
@@ -101,20 +99,20 @@
 
     def in_copy(chunk, item, color):
         owner = route(item, color)[0]
-        return pltpu.make_async_copy(piece_at(owner, color, chunk), pad_in.at[item % 2, color], pad_sem.at[item % 2, color])
+        return pltpu.make_async_copy(piece_at(owner, color, chunk), pad_in.at[item % SLOTS, color], pad_sem.at[item % SLOTS])
 
     def start_in(chunk, item):
         for color in range(COLORS):
             in_copy(chunk, item, color).start()
 
     def pack_item(chunk, item):
-        for color in range(COLORS):
-            in_copy(chunk, item, color).wait()
+        wait_bytes(pad_in.at[item % SLOTS], pad_sem.at[item % SLOTS])
+        for color in range(COLORS):
             place_owner, place_row = packed_at(packed_index(color, chunk, item))
 
             def pack(sub, inner):
                 off = pl.multiple_of(sub * SUB_ROWS * LANES, SUB_ROWS * LANES)
-                vals = pad_in[item % 2, color, :, pl.ds(off, SUB_ROWS * LANES)].astype(jnp.float32)
+                vals = pad_in[item % SLOTS, color, :, pl.ds(off, SUB_ROWS * LANES)].astype(jnp.float32)
                 to = pl.multiple_of(place_row + sub * SUB_ROWS, SUB_ROWS)
                 weights_ref[place_owner, pl.ds(to, SUB_ROWS), :] = (
                     vals.reshape(SUB_ROWS, LANES).astype(jnp.bfloat16))
@@ -133,9 +131,9 @@
 
     def pack_and_send(chunk, first):
         def one_item(item, carry):
-            @pl.when(item + 1 < ITEMS)
+            @pl.when(item + SLOTS - 1 < ITEMS)
             def _():
-                start_in(chunk, item + 1)
+                start_in(chunk, item + SLOTS - 1)
 
             pack_item(chunk, item)
             send_item(chunk, item)
@@ -143,27 +141,28 @@
 
         lax.fori_loop(first, ITEMS, one_item, 0)
 
-    def part_copies(chunk, place, color, slot):
-        flip1, flip2, flip3 = flips[color]
-        owner = me + (1 - place // 2) * flip2 + (1 - place % 2) * flip3
-        return (pltpu.make_async_copy(land_ref.at[color, chunk, place],
-                                      weights_ref.at[part_owner, pl.ds(part_at(slot, color), part_rows)],
-                                      part_sem.at[slot, color]),
-                pltpu.make_async_copy(piece_at(owner, color, chunk), pad_in.at[slot, color], pad_sem.at[slot, color]))
+    def start_parts(chunk, place):
+        slot = place % SLOTS
+        for color in range(COLORS):
+            flip1, flip2, flip3 = flips[color]
+            owner = me + (1 - place // 2) * flip2 + (1 - place % 2) * flip3
+            pltpu.make_async_copy(land_ref.at[color, chunk, place],
+                                  weights_ref.at[part_owner + slot, pl.ds(color * part_rows, part_rows)],
+                                  part_sem.at[slot]).start()
+            pltpu.make_async_copy(piece_at(owner, color, chunk), pad_in.at[slot, color], pad_sem.at[slot]).start()
 
     def first_sums(chunk):
         for color in range(COLORS):
             wait_bytes(land_ref.at[color, chunk], recv1_sem.at[color, chunk])
-            for copy in part_copies(chunk, 0, color, 0):
-                copy.start()
+        for place in range(SLOTS - 1):
+            start_parts(chunk, place)
         for place in range(4):
-            slot = place % 2
+            slot = place % SLOTS
+            if place + SLOTS - 1 < 4:
+                start_parts(chunk, place + SLOTS - 1)
+            wait_bytes(weights_ref.at[part_owner + slot, pl.ds(0, COLORS * part_rows)], part_sem.at[slot])
+            wait_bytes(pad_in.at[slot], pad_sem.at[slot])
             for color in range(COLORS):
-                if place < 3:
-                    for copy in part_copies(chunk, place + 1, color, (place + 1) % 2):
-                        copy.start()
-                for copy in part_copies(chunk, place, color, slot):
-                    copy.wait()
                 at = rows_at(color, chunk)
                 total = (new_moment_ref.at[at], new_second_ref.at[at], keep.at[chunk, color], new_master_ref.at[at])[place]
 
@@ -173,8 +172,8 @@
                     vals = pad_in[slot, color, :, pl.ds(off, SUB_ROWS * LANES)].astype(jnp.float32)
                     vals = vals.reshape(SUB_ROWS, LANES)
                     for source in range(3):
-                        row = pl.multiple_of(part_at(slot, color) + source * rows + sub * SUB_ROWS, SUB_ROWS)
-                        vals = vals + weights_ref[part_owner, pl.ds(row, SUB_ROWS), :].astype(jnp.float32)
+                        row = pl.multiple_of(color * part_rows + source * rows + sub * SUB_ROWS, SUB_ROWS)
+                        vals = vals + weights_ref[part_owner + slot, pl.ds(row, SUB_ROWS), :].astype(jnp.float32)
                     total[to, :] = vals
                     return inner
 
@@ -184,8 +183,8 @@
                         total, recv2.at[chunk, color, place], send2_sem.at[place], recv2_sem.at[color, chunk],
                         device_id=(me + flips[color][1],), device_id_type=MESH).start()
 
-    start_in(0, 0)
-    start_in(0, 1)
+    for item in range(SLOTS):
+        start_in(0, item)
     barrier = pltpu.get_barrier_semaphore()
     for neighbour in neighbours:
         pl.semaphore_signal(barrier, inc=1, device_id=(neighbour,), device_id_type=MESH)
@@ -195,7 +194,8 @@
     pack_and_send(0, 1)
 
     def pack_ahead(chunk, carry):
-        start_in(chunk, 0)
+        for item in range(SLOTS - 1):
+            start_in(chunk, item)
         pack_and_send(chunk, 0)
         return carry
 
@@ -206,7 +206,8 @@
 
         @pl.when(chunk + AHEAD < CHUNKS)
         def _():
-            start_in(chunk + AHEAD, 0)
+            for item in range(SLOTS - 1):
+                start_in(chunk + AHEAD, item)
             pack_and_send(chunk + AHEAD, 0)
 
         return carry
@@ -214,11 +215,15 @@
     lax.fori_loop(0, CHUNKS, first_stage, 0)
 
     def second_stage(chunk, carry):
-        copies = [pltpu.make_async_copy(recv2.at[chunk, color], recv2_in.at[color], recv2_in_sem.at[color])
+        copies = [pltpu.make_async_copy(recv2.at[chunk, color], recv2_in.at[color % 2], recv2_in_sem.at[color % 2])
                   for color in range(COLORS)]
-        for color in range(COLORS):
+
+        def fetch(color):
             wait_bytes(recv2.at[chunk, color], recv2_sem.at[color, chunk])
             copies[color].start()
+
+        fetch(0)
+        fetch(1)
         for color in range(COLORS):
             copies[color].wait()
             base = color * color_rows + chunk * rows
@@ -226,14 +231,16 @@
             def add(sub, inner):
                 to = pl.ds(pl.multiple_of(sub * SUB_ROWS, SUB_ROWS), SUB_ROWS)
                 out = pl.ds(pl.multiple_of(base + sub * SUB_ROWS, SUB_ROWS), SUB_ROWS)
-                keep[chunk, color, to, :] += recv2_in[color, 0, to, :]
-                new_master_ref[out, :] += recv2_in[color, 1, to, :]
+                keep[chunk, color, to, :] += recv2_in[color % 2, 0, to, :]
+                new_master_ref[out, :] += recv2_in[color % 2, 1, to, :]
                 return inner
 
             lax.fori_loop(0, rows // SUB_ROWS, add, 0)
             pltpu.make_async_remote_copy(
                 keep.at[chunk, color], recv3.at[chunk, color], send3_sem.at[chunk], recv3_sem.at[color, chunk],
                 device_id=(me + flips[color][2],), device_id_type=MESH).start()
+            if color == 0:
+                fetch(2)
         return carry
 
     second_stage(0, 0)
@@ -267,7 +274,7 @@
     def state_copies(chunk, color):
         slot = (chunk * COLORS + color) % RING
         at = rows_at(color, chunk)
-        return [pltpu.make_async_copy(ref.at[at], keep.at[slot, index], state_sem.at[slot, index])
+        return [pltpu.make_async_copy(ref.at[at], keep.at[slot, index], state_sem.at[slot])
                 for index, ref in enumerate((master_ref, moment_ref, second_ref))]
 
     lax.fori_loop(0, CHUNKS - 2, third_stage, 0)
@@ -317,8 +324,7 @@
         for color in range(COLORS):
             item = chunk * COLORS + color
             slot = item % RING
-            for copy in state_copies(chunk, color):
-                copy.wait()
+            wait_bytes(keep.at[slot], state_sem.at[slot])
             base = color * color_rows + chunk * rows
 
             def update(sub, inner):
@@ -431,14 +437,14 @@
         in_specs=[hbm_spec] * 5 + [vmem_spec] * 3,
         out_specs=(vmem_spec,) * 8 + (hbm_spec,) * 2,
         scratch_shapes=[
-            pltpu.VMEM((2, COLORS, 1, rows * LANES), bf16),
+            pltpu.VMEM((SLOTS, COLORS, 1, rows * LANES), bf16),
             pltpu.VMEM((CHUNKS, COLORS, rows, LANES), f32),
-            pltpu.VMEM((COLORS, 2, rows, LANES), f32),
+            pltpu.VMEM((2, 2, rows, LANES), f32),
             pltpu.VMEM((CHUNKS, COLORS, rows, LANES), f32),
             pltpu.VMEM((GROUP, 1, vec_share), bf16),
             pltpu.VMEM((GROUP, 1, LANES), f32),
             pltpu.VMEM((8, LANES), f32),
-            dma((2, COLORS)), dma((2, COLORS)), dma((COLORS,)), dma((RING, 3)),
+            dma((SLOTS,)), dma((SLOTS,)), dma((2,)), dma((RING,)),
             dma((CHUNKS,)), dma((2,)), dma((CHUNKS,)),
             dma((COLORS, CHUNKS)), dma((COLORS, CHUNKS)), dma((COLORS, CHUNKS)), dma((7,)),
             dma((COLORS,)), dma((7, COLORS, CHUNKS)), dma((COLORS,)), dma((COLORS,)),

time: 407 us -> 406 us (level)
  no operation moved by 1% of the time
where the time goes in v6:
time: 406 us; the launch traced here: 404 us
  Pallas kernels  404 us (100%)
    pallas_call x1, Pallas kernels, step_call(): pl.pallas_call(functools.partial(step_kernel, rows, share, vec_share), na...  386 us
    pallas_call x1, Pallas kernels, store_call(): pl.pallas_call(store_kernel, name='store_results', out_shape=tuple((jax.S...  17.9 us

profile of v6, /device:TPU:0, one launch (start us, length us, event | category | flops | bytes accessed | tf_op | source)
XLA Modules:
  0.0 404.2 jit_solution(13701211724001618991)
XLA Ops:
  0.6 385.6 %adam_step.1 = (f32[9600,128]{1,0:T(8,128)S(1)}, f32[9600,128]{1,0:T(8,128)S(1)}, f32[9600,128]{1,0:T(8,128)S(1)}, f32[1,512]{1,0:T(1,128)S(1)}, f32[1,512]{1,0:...) custom-call(bf16[1,19660800]{1,0:T(2,128)(2,1)} %grad_ref.1, ...), custom_call_target="tpu_custom_call" | custom-call | tf_op jit(solution)/shard_map/adam_step/pallas_call | solution.py:429
  386.2 17.9 %store_results.1 = (f32[9600,128]{1,0:T(8,128)}, f32[9600,128]{1,0:T(8,128)}, f32[9600,128]{1,0:T(8,128)}, f32[1,512]{1,0:T(1,128)}, f32[1,512]{1,0:T(1,128)}, /...) custom-call(f32[9600,128]{1,0:T(8,128)S(1)} %get-tuple-element.24.refs_0_, ...), custom_call_target="tpu_custom_call" | custom-call | tf_op jit(solution)/shard_map/store_results/pallas_call | solution.py:482

commit v7 on v6

--- a/solution.py
+++ b/solution.py
@@ -23,8 +23,8 @@
 LANES = 128
 ORDERS = ((2, 4, 8), (4, 8, 2), (8, 2, 4))
 COLORS = len(ORDERS)
-CHUNKS = 8
-AHEAD = 3
+CHUNKS = 10
+AHEAD = 2
 SLOTS = 3
 SUB_ROWS = 80
 UPDATE_ROWS = 80
@@ -127,7 +127,7 @@
             pltpu.make_async_remote_copy(
                 weights_ref.at[place_owner, pl.ds(place_row, rows)],
                 land_ref.at[color, chunk, place, pl.ds(pl.multiple_of(source * rows, rows), rows)],
-                send1_sem.at[chunk], recv1_sem.at[color, chunk], device_id=(target,), device_id_type=MESH).start()
+                send1_sem.at[chunk], recv1_sem.at[color, chunk, place], device_id=(target,), device_id_type=MESH).start()
 
     def pack_and_send(chunk, first):
         def one_item(item, carry):
@@ -141,47 +141,48 @@
 
         lax.fori_loop(first, ITEMS, one_item, 0)
 
-    def start_parts(chunk, place):
-        slot = place % SLOTS
-        for color in range(COLORS):
-            flip1, flip2, flip3 = flips[color]
-            owner = me + (1 - place // 2) * flip2 + (1 - place % 2) * flip3
+    def first_sums(chunk, place, pack_chunk):
+        if pack_chunk is not None:
+            for item in range(SLOTS):
+                start_in(pack_chunk, place * SLOTS + item)
+        owners = [me + (1 - place // 2) * flip2 + (1 - place % 2) * flip3 for _, flip2, flip3 in flips]
+        for color in range(COLORS):
+            pltpu.make_async_copy(piece_at(owners[color], color, chunk), pad_in.at[SLOTS, color], pad_sem.at[SLOTS]).start()
+        slot = place % 2
+        for color in range(COLORS):
+            wait_bytes(land_ref.at[color, chunk, place], recv1_sem.at[color, chunk, place])
             pltpu.make_async_copy(land_ref.at[color, chunk, place],
                                   weights_ref.at[part_owner + slot, pl.ds(color * part_rows, part_rows)],
                                   part_sem.at[slot]).start()
-            pltpu.make_async_copy(piece_at(owner, color, chunk), pad_in.at[slot, color], pad_sem.at[slot]).start()
-
-    def first_sums(chunk):
-        for color in range(COLORS):
-            wait_bytes(land_ref.at[color, chunk], recv1_sem.at[color, chunk])
-        for place in range(SLOTS - 1):
-            start_parts(chunk, place)
-        for place in range(4):
-            slot = place % SLOTS
-            if place + SLOTS - 1 < 4:
-                start_parts(chunk, place + SLOTS - 1)
-            wait_bytes(weights_ref.at[part_owner + slot, pl.ds(0, COLORS * part_rows)], part_sem.at[slot])
-            wait_bytes(pad_in.at[slot], pad_sem.at[slot])
-            for color in range(COLORS):
-                at = rows_at(color, chunk)
-                total = (new_moment_ref.at[at], new_second_ref.at[at], keep.at[chunk, color], new_master_ref.at[at])[place]
-
-                def add(sub, inner):
-                    off = pl.multiple_of(sub * SUB_ROWS * LANES, SUB_ROWS * LANES)
-                    to = pl.ds(pl.multiple_of(sub * SUB_ROWS, SUB_ROWS), SUB_ROWS)
-                    vals = pad_in[slot, color, :, pl.ds(off, SUB_ROWS * LANES)].astype(jnp.float32)
-                    vals = vals.reshape(SUB_ROWS, LANES)
-                    for source in range(3):
-                        row = pl.multiple_of(color * part_rows + source * rows + sub * SUB_ROWS, SUB_ROWS)
-                        vals = vals + weights_ref[part_owner + slot, pl.ds(row, SUB_ROWS), :].astype(jnp.float32)
-                    total[to, :] = vals
-                    return inner
-
-                lax.fori_loop(0, rows // SUB_ROWS, add, 0, unroll=True)
-                if place < 2:
-                    pltpu.make_async_remote_copy(
-                        total, recv2.at[chunk, color, place], send2_sem.at[place], recv2_sem.at[color, chunk],
-                        device_id=(me + flips[color][1],), device_id_type=MESH).start()
+        if pack_chunk is not None:
+            def one_item(item, carry):
+                pack_item(pack_chunk, item)
+                send_item(pack_chunk, item)
+                return carry
+
+            lax.fori_loop(place * SLOTS, (place + 1) * SLOTS, one_item, 0)
+        wait_bytes(pad_in.at[SLOTS], pad_sem.at[SLOTS])
+        wait_bytes(weights_ref.at[part_owner + slot, pl.ds(0, COLORS * part_rows)], part_sem.at[slot])
+        for color in range(COLORS):
+            at = rows_at(color, chunk)
+            total = (new_moment_ref.at[at], new_second_ref.at[at], keep.at[chunk, color], new_master_ref.at[at])[place]
+
+            def add(sub, inner):
+                off = pl.multiple_of(sub * SUB_ROWS * LANES, SUB_ROWS * LANES)
+                to = pl.ds(pl.multiple_of(sub * SUB_ROWS, SUB_ROWS), SUB_ROWS)
+                vals = pad_in[SLOTS, color, :, pl.ds(off, SUB_ROWS * LANES)].astype(jnp.float32)
+                vals = vals.reshape(SUB_ROWS, LANES)
+                for source in range(3):
+                    row = pl.multiple_of(color * part_rows + source * rows + sub * SUB_ROWS, SUB_ROWS)
+                    vals = vals + weights_ref[part_owner + slot, pl.ds(row, SUB_ROWS), :].astype(jnp.float32)
+                total[to, :] = vals
+                return inner
+
+            lax.fori_loop(0, rows // SUB_ROWS, add, 0, unroll=True)
+            if place < 2:
+                pltpu.make_async_remote_copy(
+                    total, recv2.at[chunk, color, place], send2_sem.at[place], recv2_sem.at[color, chunk],
+                    device_id=(me + flips[color][1],), device_id_type=MESH).start()
 
     for item in range(SLOTS):
         start_in(0, item)
@@ -202,45 +203,37 @@
     lax.fori_loop(1, AHEAD, pack_ahead, 0)
 
     def first_stage(chunk, carry):
-        first_sums(chunk)
-
-        @pl.when(chunk + AHEAD < CHUNKS)
-        def _():
-            for item in range(SLOTS - 1):
-                start_in(chunk + AHEAD, item)
-            pack_and_send(chunk + AHEAD, 0)
-
-        return carry
-
-    lax.fori_loop(0, CHUNKS, first_stage, 0)
+        for place in range(4):
+            first_sums(chunk, place, chunk + AHEAD)
+        return carry
+
+    def first_stage_last(chunk, carry):
+        for place in range(4):
+            first_sums(chunk, place, None)
+        return carry
+
+    lax.fori_loop(0, CHUNKS - AHEAD, first_stage, 0)
+    lax.fori_loop(CHUNKS - AHEAD, CHUNKS, first_stage_last, 0)
 
     def second_stage(chunk, carry):
-        copies = [pltpu.make_async_copy(recv2.at[chunk, color], recv2_in.at[color % 2], recv2_in_sem.at[color % 2])
-                  for color in range(COLORS)]
-
-        def fetch(color):
+        for color in range(COLORS):
             wait_bytes(recv2.at[chunk, color], recv2_sem.at[color, chunk])
-            copies[color].start()
-
-        fetch(0)
-        fetch(1)
-        for color in range(COLORS):
-            copies[color].wait()
+            copy = pltpu.make_async_copy(recv2.at[chunk, color], recv2_in, recv2_in_sem)
+            copy.start()
+            copy.wait()
             base = color * color_rows + chunk * rows
 
             def add(sub, inner):
                 to = pl.ds(pl.multiple_of(sub * SUB_ROWS, SUB_ROWS), SUB_ROWS)
                 out = pl.ds(pl.multiple_of(base + sub * SUB_ROWS, SUB_ROWS), SUB_ROWS)
-                keep[chunk, color, to, :] += recv2_in[color % 2, 0, to, :]
-                new_master_ref[out, :] += recv2_in[color % 2, 1, to, :]
+                keep[chunk, color, to, :] += recv2_in[0, to, :]
+                new_master_ref[out, :] += recv2_in[1, to, :]
                 return inner
 
-            lax.fori_loop(0, rows // SUB_ROWS, add, 0)
+            lax.fori_loop(0, rows // SUB_ROWS, add, 0, unroll=True)
             pltpu.make_async_remote_copy(
                 keep.at[chunk, color], recv3.at[chunk, color], send3_sem.at[chunk], recv3_sem.at[color, chunk],
                 device_id=(me + flips[color][2],), device_id_type=MESH).start()
-            if color == 0:
-                fetch(2)
         return carry
 
     second_stage(0, 0)
@@ -437,16 +430,16 @@
         in_specs=[hbm_spec] * 5 + [vmem_spec] * 3,
         out_specs=(vmem_spec,) * 8 + (hbm_spec,) * 2,
         scratch_shapes=[
-            pltpu.VMEM((SLOTS, COLORS, 1, rows * LANES), bf16),
+            pltpu.VMEM((SLOTS + 1, COLORS, 1, rows * LANES), bf16),
             pltpu.VMEM((CHUNKS, COLORS, rows, LANES), f32),
-            pltpu.VMEM((2, 2, rows, LANES), f32),
+            pltpu.VMEM((2, rows, LANES), f32),
             pltpu.VMEM((CHUNKS, COLORS, rows, LANES), f32),
             pltpu.VMEM((GROUP, 1, vec_share), bf16),
             pltpu.VMEM((GROUP, 1, LANES), f32),
             pltpu.VMEM((8, LANES), f32),
-            dma((SLOTS,)), dma((SLOTS,)), dma((2,)), dma((RING,)),
+            dma((SLOTS + 1,)), dma((2,)), dma, dma((RING,)),
             dma((CHUNKS,)), dma((2,)), dma((CHUNKS,)),
-            dma((COLORS, CHUNKS)), dma((COLORS, CHUNKS)), dma((COLORS, CHUNKS)), dma((7,)),
+            dma((COLORS, CHUNKS, 4)), dma((COLORS, CHUNKS)), dma((COLORS, CHUNKS)), dma((7,)),
             dma((COLORS,)), dma((7, COLORS, CHUNKS)), dma((COLORS,)), dma((COLORS,)),
         ],
         compiler_params=pltpu.CompilerParams(

time: 406 us -> 408 us (level)
  no operation moved by 1% of the time
where the time goes in v7:
time: 408 us; the launch traced here: 405 us
  Pallas kernels  405 us (99%)
    pallas_call x1, Pallas kernels, step_call(): pl.pallas_call(functools.partial(step_kernel, rows, share, vec_share), na...  387 us
    pallas_call x1, Pallas kernels, store_call(): pl.pallas_call(store_kernel, name='store_results', out_shape=tuple((jax.S...  17.9 us

profile of v7, /device:TPU:0, one launch (start us, length us, event | category | flops | bytes accessed | tf_op | source)
XLA Modules:
  0.0 405.3 jit_solution(11444443757765237133)
XLA Ops:
  0.6 386.8 %adam_step.1 = (f32[9600,128]{1,0:T(8,128)S(1)}, f32[9600,128]{1,0:T(8,128)S(1)}, f32[9600,128]{1,0:T(8,128)S(1)}, f32[1,512]{1,0:T(1,128)S(1)}, f32[1,512]{1,0:...) custom-call(bf16[1,19660800]{1,0:T(2,128)(2,1)} %grad_ref.1, ...), custom_call_target="tpu_custom_call" | custom-call | tf_op jit(solution)/shard_map/adam_step/pallas_call | solution.py:422
  387.4 17.9 %store_results.1 = (f32[9600,128]{1,0:T(8,128)}, f32[9600,128]{1,0:T(8,128)}, f32[9600,128]{1,0:T(8,128)}, f32[1,512]{1,0:T(1,128)}, f32[1,512]{1,0:T(1,128)}, /...) custom-call(f32[9600,128]{1,0:T(8,128)S(1)} %get-tuple-element.24.refs_0_, ...), custom_call_target="tpu_custom_call" | custom-call | tf_op jit(solution)/shard_map/store_results/pallas_call | solution.py:475

commit v8 on v6

--- a/solution.py
+++ b/solution.py
@@ -26,6 +26,7 @@
 CHUNKS = 8
 AHEAD = 3
 SLOTS = 3
+PIECES = 4
 SUB_ROWS = 80
 UPDATE_ROWS = 80
 RING = 4
@@ -308,19 +309,24 @@
     norm = jnp.sqrt(jnp.sum(jnp.sum(square_land[...], axis=0), axis=1, keepdims=True))
     clip_coef = jnp.minimum(1.0, 1.0 / (norm + NORM_EPS))
 
-    def link_copy(stage, owner, color, chunk, hop, part=None):
-        piece = weights_ref.at[owner, rows_at(color, chunk) if part is None else part]
+    piece_rows = CHUNKS * rows // PIECES
+
+    def piece_rows_at(color, piece):
+        return pl.ds(pl.multiple_of(color * color_rows + piece * piece_rows, piece_rows), piece_rows)
+
+    def link_copy(stage, owner, color, piece, hop, part=None):
+        place = weights_ref.at[owner, piece_rows_at(color, piece) if part is None else part]
         return pltpu.make_async_remote_copy(
-            piece, piece, send_sem.at[color], recv_sem.at[stage, color, chunk],
+            place, place, send_sem.at[color], recv_sem.at[stage, color, piece],
             device_id=(me + flips[color][hop],), device_id_type=MESH)
 
-    def core_copy(owner, color, chunk):
-        piece = weights_ref.at[owner, rows_at(color, chunk)]
+    def core_copy(owner, color, piece):
+        place = weights_ref.at[owner, piece_rows_at(color, piece)]
         return pltpu.make_async_remote_copy(
-            piece, piece, core_send_sem.at[color], core_recv_sem.at[color],
+            place, place, core_send_sem.at[color], core_recv_sem.at[color],
             device_id=(partner,), device_id_type=MESH)
 
-    def update_chunk(chunk, first):
+    def update_chunk(chunk, form):
         for color in range(COLORS):
             item = chunk * COLORS + color
             slot = item % RING
@@ -337,48 +343,53 @@
                 new_moment_ref[out, :] = moment
                 new_second_ref[out, :] = second
                 weights_ref[me, out, :] = master.astype(jnp.bfloat16)
-                if first:
+                if form == 'parts':
                     for stage, hop in ((0, 0), (1, 1), (3, 2)):
-                        link_copy(stage, me, color, chunk, hop, out).start()
+                        link_copy(stage, me, color, 0, hop, out).start()
                 return inner
 
             lax.fori_loop(0, rows // UPDATE_ROWS, update, 0)
-            if not first:
-                link_copy(0, me, color, chunk, 0).start()
+            if form == 'chunk':
+                for stage, hop in ((0, 0), (1, 1), (3, 2)):
+                    link_copy(stage, me, color, 0, hop, rows_at(color, chunk)).start()
+            if form == 'piece':
+                link_copy(0, me, color, chunk // 2, 0).start()
 
             @pl.when(item + RING < CHUNKS * COLORS)
             def _():
                 for copy in state_copies((item + RING) // COLORS, (item + RING) % COLORS):
                     copy.start()
 
-    def update_later(chunk, carry):
-        update_chunk(chunk, False)
-        return carry
-
-    update_chunk(0, True)
-    lax.fori_loop(1, CHUNKS, update_later, 0)
+    def update_later(piece, carry):
+        update_chunk(piece * 2, None)
+        update_chunk(piece * 2 + 1, 'piece')
+        return carry
+
+    update_chunk(0, 'parts')
+    update_chunk(1, 'chunk')
+    lax.fori_loop(1, PIECES, update_later, 0)
 
     vec_new = adam_update(vec_sum, clip_coef, vec_master_ref[...], vec_moment_ref[...], vec_second_ref[...], 0.0)
     vec_new_master_ref[...], vec_new_moment_ref[...], vec_new_second_ref[...] = vec_new
     vec_weights_ref[me] = vec_new[0].reshape(vec_share // LANES, LANES)
 
-    def own_sends(chunk, carry):
-        for color in range(COLORS):
-            @pl.when(chunk > 0)
+    def own_sends(piece, carry):
+        for color in range(COLORS):
+            @pl.when(piece > 0)
             def _():
-                link_copy(1, me, color, chunk, 1).start()
-
-            core_copy(me, color, chunk).start()
-        return carry
-
-    lax.fori_loop(0, CHUNKS, own_sends, 0)
-
-    def own_sends_last(chunk, carry):
-        for color in range(COLORS):
-            link_copy(3, me, color, chunk, 2).start()
-        return carry
-
-    lax.fori_loop(1, CHUNKS, own_sends_last, 0)
+                link_copy(1, me, color, piece, 1).start()
+
+            core_copy(me, color, piece).start()
+        return carry
+
+    lax.fori_loop(0, PIECES, own_sends, 0)
+
+    def own_sends_last(piece, carry):
+        for color in range(COLORS):
+            link_copy(3, me, color, piece, 2).start()
+        return carry
+
+    lax.fori_loop(1, PIECES, own_sends_last, 0)
 
     for other in others:
         pltpu.make_async_remote_copy(
@@ -386,16 +397,16 @@
             device_id=(other,), device_id_type=MESH).start()
 
     def arrivals(stage, hops, onward):
-        def one_chunk(chunk, carry):
+        def one_piece(piece, carry):
             for color in range(COLORS):
                 owner = me + sum(flips[color][hop] for hop in hops)
-                wait_bytes(weights_ref.at[owner, rows_at(color, chunk)], recv_sem.at[stage, color, chunk])
+                wait_bytes(weights_ref.at[owner, piece_rows_at(color, piece)], recv_sem.at[stage, color, piece])
                 for next_stage, hop in onward:
-                    link_copy(next_stage, owner, color, chunk, hop).start()
-                core_copy(owner, color, chunk).start()
+                    link_copy(next_stage, owner, color, piece, hop).start()
+                core_copy(owner, color, piece).start()
             return carry
 
-        lax.fori_loop(0, CHUNKS, one_chunk, 0)
+        lax.fori_loop(0, PIECES, one_piece, 0)
 
     arrivals(0, (0,), ((2, 1), (4, 2)))
     arrivals(1, (1,), ((5, 2),))
@@ -447,7 +458,7 @@
             dma((SLOTS,)), dma((SLOTS,)), dma((2,)), dma((RING,)),
             dma((CHUNKS,)), dma((2,)), dma((CHUNKS,)),
             dma((COLORS, CHUNKS)), dma((COLORS, CHUNKS)), dma((COLORS, CHUNKS)), dma((7,)),
-            dma((COLORS,)), dma((7, COLORS, CHUNKS)), dma((COLORS,)), dma((COLORS,)),
+            dma((COLORS,)), dma((7, COLORS, PIECES)), dma((COLORS,)), dma((COLORS,)),
         ],
         compiler_params=pltpu.CompilerParams(
             collective_id=0, has_side_effects=True, vmem_limit_bytes=SCRATCH_BYTES),

time: 406 us -> 406 us (level)
  no operation moved by 1% of the time
where the time goes in v8:
time: 406 us; the launch traced here: 404 us
  Pallas kernels  403 us (99%)
    pallas_call x1, Pallas kernels, step_call(): pl.pallas_call(functools.partial(step_kernel, rows, share, vec_share), na...  385 us
    pallas_call x1, Pallas kernels, store_call(): pl.pallas_call(store_kernel, name='store_results', out_shape=tuple((jax.S...  17.9 us

profile of v8, /device:TPU:0, one launch (start us, length us, event | category | flops | bytes accessed | tf_op | source)
XLA Modules:
  0.0 403.8 jit_solution(10441529822721577753)
XLA Ops:
  0.6 385.3 %adam_step.1 = (f32[9600,128]{1,0:T(8,128)S(1)}, f32[9600,128]{1,0:T(8,128)S(1)}, f32[9600,128]{1,0:T(8,128)S(1)}, f32[1,512]{1,0:T(1,128)S(1)}, f32[1,512]{1,0:...) custom-call(bf16[1,19660800]{1,0:T(2,128)(2,1)} %grad_ref.1, ...), custom_call_target="tpu_custom_call" | custom-call | tf_op jit(solution)/shard_map/adam_step/pallas_call | solution.py:440
  385.9 17.9 %store_results.1 = (f32[9600,128]{1,0:T(8,128)}, f32[9600,128]{1,0:T(8,128)}, f32[9600,128]{1,0:T(8,128)}, f32[1,512]{1,0:T(1,128)}, f32[1,512]{1,0:T(1,128)}, /...) custom-call(f32[9600,128]{1,0:T(8,128)S(1)} %get-tuple-element.24.refs_0_, ...), custom_call_target="tpu_custom_call" | custom-call | tf_op jit(solution)/shard_map/store_results/pallas_call | solution.py:493

commit v9 on v8

--- a/solution.py
+++ b/solution.py
@@ -24,7 +24,7 @@
 ORDERS = ((2, 4, 8), (4, 8, 2), (8, 2, 4))
 COLORS = len(ORDERS)
 CHUNKS = 8
-AHEAD = 3
+AHEAD = 2
 SLOTS = 3
 PIECES = 4
 SUB_ROWS = 80
@@ -64,7 +64,8 @@
     color_len = share // COLORS
     color_rows = color_len // LANES
     flips = [[flip_of(me, bit) for bit in order] for order in ORDERS]
-    per_owner = share // LANES // rows
+    piece_rows = CHUNKS * rows // PIECES
+    per_owner = share // LANES // piece_rows
     neighbours = [partner] + [me + flip_of(me, bit) + other for bit in ORDERS[0] for other in (0, flip_of(me, 1))]
     others = [me + sum(flip_of(me, bit) for bit in (1, 2, 4, 8) if mask & bit)
               for mask in sorted(range(1, GROUP), key=lambda mask: (-(mask >> 1).bit_count(), mask))]
@@ -79,13 +80,11 @@
         start = pl.multiple_of(owner * share + color * color_len + chunk * block, block)
         return grad_ref.at[:, pl.ds(start, block)]
 
-    def packed_at(index):
-        return index // per_owner, pl.multiple_of((index % per_owner) * rows, rows)
-
-    def packed_index(color, chunk, item):
-        return (chunk * COLORS + color) * ITEMS + item
-
-    part_owner = COLORS * CHUNKS * ITEMS // per_owner
+    def packed_at(color, piece, item):
+        index = (piece * COLORS + color) * ITEMS + item
+        return index // per_owner, pl.multiple_of((index % per_owner) * piece_rows, piece_rows)
+
+    part_owner = COLORS * PIECES * ITEMS // per_owner
     part_rows = 3 * rows
 
     def route(item, color):
@@ -98,63 +97,68 @@
         source = (1 - local) * (1 + core)
         return owner, target, source, place
 
-    def in_copy(chunk, item, color):
-        owner = route(item, color)[0]
-        return pltpu.make_async_copy(piece_at(owner, color, chunk), pad_in.at[item % SLOTS, color], pad_sem.at[item % SLOTS])
-
-    def start_in(chunk, item):
-        for color in range(COLORS):
-            in_copy(chunk, item, color).start()
-
-    def pack_item(chunk, item):
-        wait_bytes(pad_in.at[item % SLOTS], pad_sem.at[item % SLOTS])
-        for color in range(COLORS):
-            place_owner, place_row = packed_at(packed_index(color, chunk, item))
+    def start_in(piece, step):
+        for color in range(COLORS):
+            owner = route(step // 2, color)[0]
+            pltpu.make_async_copy(piece_at(owner, color, piece * 2 + step % 2), pad_in.at[step % SLOTS, color],
+                                  pad_sem.at[step % SLOTS]).start()
+
+    def pack_step(piece, step):
+        wait_bytes(pad_in.at[step % SLOTS], pad_sem.at[step % SLOTS])
+        for color in range(COLORS):
+            place_owner, place_row = packed_at(color, piece, step // 2)
 
             def pack(sub, inner):
                 off = pl.multiple_of(sub * SUB_ROWS * LANES, SUB_ROWS * LANES)
-                vals = pad_in[item % SLOTS, color, :, pl.ds(off, SUB_ROWS * LANES)].astype(jnp.float32)
-                to = pl.multiple_of(place_row + sub * SUB_ROWS, SUB_ROWS)
+                vals = pad_in[step % SLOTS, color, :, pl.ds(off, SUB_ROWS * LANES)].astype(jnp.float32)
+                to = pl.multiple_of(place_row + (step % 2) * rows + sub * SUB_ROWS, SUB_ROWS)
                 weights_ref[place_owner, pl.ds(to, SUB_ROWS), :] = (
                     vals.reshape(SUB_ROWS, LANES).astype(jnp.bfloat16))
                 return inner
 
             lax.fori_loop(0, rows // SUB_ROWS, pack, 0, unroll=True)
 
-    def send_item(chunk, item):
+    def send_item(piece, item, start=0, size=None):
+        size = piece_rows if size is None else size
         for color in range(COLORS):
             owner, target, source, place = route(item, color)
-            place_owner, place_row = packed_at(packed_index(color, chunk, item))
+            place_owner, place_row = packed_at(color, piece, item)
+            from_row = pl.multiple_of(place_row + start, rows)
+            to_row = pl.multiple_of(source * piece_rows + start, rows)
             pltpu.make_async_remote_copy(
-                weights_ref.at[place_owner, pl.ds(place_row, rows)],
-                land_ref.at[color, chunk, place, pl.ds(pl.multiple_of(source * rows, rows), rows)],
-                send1_sem.at[chunk], recv1_sem.at[color, chunk], device_id=(target,), device_id_type=MESH).start()
-
-    def pack_and_send(chunk, first):
-        def one_item(item, carry):
-            @pl.when(item + SLOTS - 1 < ITEMS)
+                weights_ref.at[place_owner, pl.ds(from_row, size)],
+                land_ref.at[color, piece, place, pl.ds(to_row, size)],
+                send1_sem.at[piece], recv1_sem.at[color, piece], device_id=(target,), device_id_type=MESH).start()
+
+    def pack_and_send(piece, first):
+        def one_step(step, carry):
+            @pl.when(step + SLOTS - 1 < 2 * ITEMS)
             def _():
-                start_in(chunk, item + SLOTS - 1)
-
-            pack_item(chunk, item)
-            send_item(chunk, item)
+                start_in(piece, step + SLOTS - 1)
+
+            pack_step(piece, step)
+
+            @pl.when(step % 2 == 1)
+            def _():
+                send_item(piece, step // 2)
+
             return carry
 
-        lax.fori_loop(first, ITEMS, one_item, 0)
+        lax.fori_loop(first, 2 * ITEMS, one_step, 0)
 
     def start_parts(chunk, place):
         slot = place % SLOTS
         for color in range(COLORS):
             flip1, flip2, flip3 = flips[color]
             owner = me + (1 - place // 2) * flip2 + (1 - place % 2) * flip3
-            pltpu.make_async_copy(land_ref.at[color, chunk, place],
-                                  weights_ref.at[part_owner + slot, pl.ds(color * part_rows, part_rows)],
-                                  part_sem.at[slot]).start()
+            for source in range(3):
+                row = pl.multiple_of(source * piece_rows + (chunk % 2) * rows, rows)
+                pltpu.make_async_copy(land_ref.at[color, chunk // 2, place, pl.ds(row, rows)],
+                                      weights_ref.at[part_owner + slot, pl.ds(color * part_rows + source * rows, rows)],
+                                      part_sem.at[slot]).start()
             pltpu.make_async_copy(piece_at(owner, color, chunk), pad_in.at[slot, color], pad_sem.at[slot]).start()
 
     def first_sums(chunk):
-        for color in range(COLORS):
-            wait_bytes(land_ref.at[color, chunk], recv1_sem.at[color, chunk])
         for place in range(SLOTS - 1):
             start_parts(chunk, place)
         for place in range(4):
@@ -184,36 +188,46 @@
                         total, recv2.at[chunk, color, place], send2_sem.at[place], recv2_sem.at[color, chunk],
                         device_id=(me + flips[color][1],), device_id_type=MESH).start()
 
-    for item in range(SLOTS):
-        start_in(0, item)
+    for step in range(SLOTS):
+        start_in(0, step)
     barrier = pltpu.get_barrier_semaphore()
     for neighbour in neighbours:
         pl.semaphore_signal(barrier, inc=1, device_id=(neighbour,), device_id_type=MESH)
-    pack_item(0, 0)
+    pack_step(0, 0)
     pl.semaphore_wait(barrier, len(neighbours))
-    send_item(0, 0)
-    pack_and_send(0, 1)
-
-    def pack_ahead(chunk, carry):
-        for item in range(SLOTS - 1):
-            start_in(chunk, item)
-        pack_and_send(chunk, 0)
+    send_item(0, 0, 0, rows)
+    start_in(0, SLOTS)
+    pack_step(0, 1)
+    send_item(0, 0, rows, rows)
+    pack_and_send(0, 2)
+
+    def pack_ahead(piece, carry):
+        for step in range(SLOTS - 1):
+            start_in(piece, step)
+        pack_and_send(piece, 0)
         return carry
 
     lax.fori_loop(1, AHEAD, pack_ahead, 0)
 
-    def first_stage(chunk, carry):
-        first_sums(chunk)
-
-        @pl.when(chunk + AHEAD < CHUNKS)
+    def first_stage(piece, carry):
+        for color in range(COLORS):
+            wait_bytes(land_ref.at[color, piece], recv1_sem.at[color, piece])
+
+        def one_chunk(chunk, inner):
+            first_sums(chunk)
+            return inner
+
+        lax.fori_loop(2 * piece, 2 * piece + 2, one_chunk, 0)
+
+        @pl.when(piece + AHEAD < PIECES)
         def _():
-            for item in range(SLOTS - 1):
-                start_in(chunk + AHEAD, item)
-            pack_and_send(chunk + AHEAD, 0)
-
-        return carry
-
-    lax.fori_loop(0, CHUNKS, first_stage, 0)
+            for step in range(SLOTS - 1):
+                start_in(piece + AHEAD, step)
+            pack_and_send(piece + AHEAD, 0)
+
+        return carry
+
+    lax.fori_loop(0, PIECES, first_stage, 0)
 
     def second_stage(chunk, carry):
         copies = [pltpu.make_async_copy(recv2.at[chunk, color], recv2_in.at[color % 2], recv2_in_sem.at[color % 2])
@@ -291,11 +305,11 @@
     vec_sum = jnp.sum(vec_land[...].astype(jnp.float32), axis=0)
     vec_square = sum(vec_sum[:, part * LANES:(part + 1) * LANES] ** 2 for part in range(vec_share // LANES))
 
-    def wait_packed(chunk, carry):
-        wait_bytes(weights_ref.at[pl.ds(0, COLORS), pl.ds(0, ITEMS * rows)], send1_sem.at[chunk])
-        return carry
-
-    lax.fori_loop(0, CHUNKS, wait_packed, 0)
+    def wait_packed(piece, carry):
+        wait_bytes(weights_ref.at[pl.ds(0, COLORS), pl.ds(0, ITEMS * piece_rows)], send1_sem.at[piece])
+        return carry
+
+    lax.fori_loop(0, PIECES, wait_packed, 0)
     third_stage(CHUNKS - 1, 0)
     square_land[me] = jnp.sum(square_acc[...], axis=0, keepdims=True) + vec_square
 
@@ -308,8 +322,6 @@
     wait_bytes(square_land.at[pl.ds(0, GROUP - 1)], small_sem.at[4])
     norm = jnp.sqrt(jnp.sum(jnp.sum(square_land[...], axis=0), axis=1, keepdims=True))
     clip_coef = jnp.minimum(1.0, 1.0 / (norm + NORM_EPS))
-
-    piece_rows = CHUNKS * rows // PIECES
 
     def piece_rows_at(color, piece):
         return pl.ds(pl.multiple_of(color * color_rows + piece * piece_rows, piece_rows), piece_rows)
@@ -443,7 +455,7 @@
         out_shape=(pltpu.VMEM((share // LANES, LANES), f32),) * 3 + (pltpu.VMEM((1, vec_share), f32),) * 3 + (
             pltpu.VMEM((GROUP, share // LANES, LANES), bf16),
             pltpu.VMEM((GROUP, vec_share // LANES, LANES), f32),
-            jax.ShapeDtypeStruct((COLORS, CHUNKS, 4, 3 * rows, LANES), bf16),
+            jax.ShapeDtypeStruct((COLORS, PIECES, 4, 3 * CHUNKS * rows // PIECES, LANES), bf16),
             jax.ShapeDtypeStruct((CHUNKS, COLORS, 2, rows, LANES), f32)),
         in_specs=[hbm_spec] * 5 + [vmem_spec] * 3,
         out_specs=(vmem_spec,) * 8 + (hbm_spec,) * 2,
@@ -456,8 +468,8 @@
             pltpu.VMEM((GROUP, 1, LANES), f32),
             pltpu.VMEM((8, LANES), f32),
             dma((SLOTS,)), dma((SLOTS,)), dma((2,)), dma((RING,)),
-            dma((CHUNKS,)), dma((2,)), dma((CHUNKS,)),
-            dma((COLORS, CHUNKS)), dma((COLORS, CHUNKS)), dma((COLORS, CHUNKS)), dma((7,)),
+            dma((PIECES,)), dma((2,)), dma((CHUNKS,)),
+            dma((COLORS, PIECES)), dma((COLORS, CHUNKS)), dma((COLORS, CHUNKS)), dma((7,)),
             dma((COLORS,)), dma((7, COLORS, PIECES)), dma((COLORS,)), dma((COLORS,)),
         ],
         compiler_params=pltpu.CompilerParams(

time: 406 us -> 405 us (level)
  no operation moved by 1% of the time
where the time goes in v9:
time: 405 us; the launch traced here: 404 us
  Pallas kernels  403 us (100%)
    pallas_call x1, Pallas kernels, step_call(): pl.pallas_call(functools.partial(step_kernel, rows, share, vec_share), na...  385 us
    pallas_call x1, Pallas kernels, store_call(): pl.pallas_call(store_kernel, name='store_results', out_shape=tuple((jax.S...  17.9 us

profile of v9, /device:TPU:0, one launch (start us, length us, event | category | flops | bytes accessed | tf_op | source)
XLA Modules:
  0.0 403.7 jit_solution(3635040696511205220)
XLA Ops:
  0.6 385.1 %adam_step.1 = (f32[9600,128]{1,0:T(8,128)S(1)}, f32[9600,128]{1,0:T(8,128)S(1)}, f32[9600,128]{1,0:T(8,128)S(1)}, f32[1,512]{1,0:T(1,128)S(1)}, f32[1,512]{1,0:...) custom-call(bf16[1,19660800]{1,0:T(2,128)(2,1)} %grad_ref.1, ...), custom_call_target="tpu_custom_call" | custom-call | tf_op jit(solution)/shard_map/adam_step/pallas_call | solution.py:452
  385.8 17.9 %store_results.1 = (f32[9600,128]{1,0:T(8,128)}, f32[9600,128]{1,0:T(8,128)}, f32[9600,128]{1,0:T(8,128)}, f32[1,512]{1,0:T(1,128)}, f32[1,512]{1,0:T(1,128)}, /...) custom-call(f32[9600,128]{1,0:T(8,128)S(1)} %get-tuple-element.24.refs_0_, ...), custom_call_target="tpu_custom_call" | custom-call | tf_op jit(solution)/shard_map/store_results/pallas_call | solution.py:505

commit v10 on v9

--- a/solution.py
+++ b/solution.py
@@ -27,6 +27,7 @@
 AHEAD = 2
 SLOTS = 3
 PIECES = 4
+IN_FLIGHT = 8
 SUB_ROWS = 80
 UPDATE_ROWS = 80
 RING = 4
@@ -128,13 +129,20 @@
             pltpu.make_async_remote_copy(
                 weights_ref.at[place_owner, pl.ds(from_row, size)],
                 land_ref.at[color, piece, place, pl.ds(to_row, size)],
-                send1_sem.at[piece], recv1_sem.at[color, piece], device_id=(target,), device_id_type=MESH).start()
+                send1_sem.at[(piece * ITEMS + item) % IN_FLIGHT], recv1_sem.at[color, piece], device_id=(target,), device_id_type=MESH).start()
+
+    def wait_left(index):
+        wait_bytes(weights_ref.at[0, pl.ds(0, COLORS * piece_rows)], send1_sem.at[index])
 
     def pack_and_send(piece, first):
         def one_step(step, carry):
             @pl.when(step + SLOTS - 1 < 2 * ITEMS)
             def _():
                 start_in(piece, step + SLOTS - 1)
+
+            @pl.when(piece * ITEMS + step // 2 - (step % 2) * ITEMS * PIECES >= IN_FLIGHT)
+            def _():
+                wait_left((piece * ITEMS + step // 2) % IN_FLIGHT)
 
             pack_step(piece, step)
 
@@ -305,11 +313,8 @@
     vec_sum = jnp.sum(vec_land[...].astype(jnp.float32), axis=0)
     vec_square = sum(vec_sum[:, part * LANES:(part + 1) * LANES] ** 2 for part in range(vec_share // LANES))
 
-    def wait_packed(piece, carry):
-        wait_bytes(weights_ref.at[pl.ds(0, COLORS), pl.ds(0, ITEMS * piece_rows)], send1_sem.at[piece])
-        return carry
-
-    lax.fori_loop(0, PIECES, wait_packed, 0)
+    for index in range(IN_FLIGHT):
+        wait_left(index)
     third_stage(CHUNKS - 1, 0)
     square_land[me] = jnp.sum(square_acc[...], axis=0, keepdims=True) + vec_square
 
@@ -468,7 +473,7 @@
             pltpu.VMEM((GROUP, 1, LANES), f32),
             pltpu.VMEM((8, LANES), f32),
             dma((SLOTS,)), dma((SLOTS,)), dma((2,)), dma((RING,)),
-            dma((PIECES,)), dma((2,)), dma((CHUNKS,)),
+            dma((IN_FLIGHT,)), dma((2,)), dma((CHUNKS,)),
             dma((COLORS, PIECES)), dma((COLORS, CHUNKS)), dma((COLORS, CHUNKS)), dma((7,)),
             dma((COLORS,)), dma((7, COLORS, PIECES)), dma((COLORS,)), dma((COLORS,)),
         ],

time: 405 us -> 405 us (level)
  no operation moved by 1% of the time
where the time goes in v10:
time: 405 us; the launch traced here: 404 us
  Pallas kernels  403 us (100%)
    pallas_call x1, Pallas kernels, step_call(): pl.pallas_call(functools.partial(step_kernel, rows, share, vec_share), na...  385 us
    pallas_call x1, Pallas kernels, store_call(): pl.pallas_call(store_kernel, name='store_results', out_shape=tuple((jax.S...  17.9 us

profile of v10, /device:TPU:0, one launch (start us, length us, event | category | flops | bytes accessed | tf_op | source)
XLA Modules:
  0.0 403.7 jit_solution(10535167285313287173)
XLA Ops:
  0.6 385.2 %adam_step.1 = (f32[9600,128]{1,0:T(8,128)S(1)}, f32[9600,128]{1,0:T(8,128)S(1)}, f32[9600,128]{1,0:T(8,128)S(1)}, f32[1,512]{1,0:T(1,128)S(1)}, f32[1,512]{1,0:...) custom-call(bf16[1,19660800]{1,0:T(2,128)(2,1)} %grad_ref.1, ...), custom_call_target="tpu_custom_call" | custom-call | tf_op jit(solution)/shard_map/adam_step/pallas_call | solution.py:457
  385.8 17.9 %store_results.1 = (f32[9600,128]{1,0:T(8,128)}, f32[9600,128]{1,0:T(8,128)}, f32[9600,128]{1,0:T(8,128)}, f32[1,512]{1,0:T(1,128)}, f32[1,512]{1,0:T(1,128)}, /...) custom-call(f32[9600,128]{1,0:T(8,128)S(1)} %get-tuple-element.24.refs_0_, ...), custom_call_target="tpu_custom_call" | custom-call | tf_op jit(solution)/shard_map/store_results/pallas_call | solution.py:510

commit v11 on v10

--- a/solution.py
+++ b/solution.py
@@ -54,9 +54,9 @@
                 new_master_ref, new_moment_ref, new_second_ref,
                 vec_new_master_ref, vec_new_moment_ref, vec_new_second_ref, weights_ref, vec_weights_ref,
                 land_ref, recv2,
-                pad_in, keep, recv2_in, recv3, vec_land, square_land, square_acc,
+                pad_in, keep, recv2_in, recv3, vec_land, vec_state, square_land, square_acc,
                 pad_sem, part_sem, recv2_in_sem, state_sem,
-                send1_sem, send2_sem, send3_sem, recv1_sem, recv2_sem, recv3_sem, small_sem,
+                send1_sem, send2_sem, send3_sem, recv1_sem, recv2_sem, recv3_sem, small_sem, vec_state_sem,
                 send_sem, recv_sem, core_send_sem, core_recv_sem):
     me = lax.axis_index(AXIS)
     core = me % 2
@@ -274,6 +274,8 @@
     vec_own = pltpu.make_async_copy(
         vec_ref.at[:, pl.ds(pl.multiple_of(me * vec_share, vec_share), vec_share)], vec_land.at[me], small_sem.at[2])
     vec_own.start()
+    for index, ref in enumerate((vec_master_ref, vec_moment_ref, vec_second_ref)):
+        pltpu.make_async_copy(ref, vec_state.at[index], vec_state_sem).start()
     lax.fori_loop(1, CHUNKS, second_stage, 0)
 
     square_acc[...] = jnp.zeros_like(square_acc)
@@ -386,7 +388,8 @@
     update_chunk(1, 'chunk')
     lax.fori_loop(1, PIECES, update_later, 0)
 
-    vec_new = adam_update(vec_sum, clip_coef, vec_master_ref[...], vec_moment_ref[...], vec_second_ref[...], 0.0)
+    wait_bytes(vec_state, vec_state_sem)
+    vec_new = adam_update(vec_sum, clip_coef, vec_state[0], vec_state[1], vec_state[2], 0.0)
     vec_new_master_ref[...], vec_new_moment_ref[...], vec_new_second_ref[...] = vec_new
     vec_weights_ref[me] = vec_new[0].reshape(vec_share // LANES, LANES)
 
@@ -462,7 +465,7 @@
             pltpu.VMEM((GROUP, vec_share // LANES, LANES), f32),
             jax.ShapeDtypeStruct((COLORS, PIECES, 4, 3 * CHUNKS * rows // PIECES, LANES), bf16),
             jax.ShapeDtypeStruct((CHUNKS, COLORS, 2, rows, LANES), f32)),
-        in_specs=[hbm_spec] * 5 + [vmem_spec] * 3,
+        in_specs=[hbm_spec] * 8,
         out_specs=(vmem_spec,) * 8 + (hbm_spec,) * 2,
         scratch_shapes=[
             pltpu.VMEM((SLOTS, COLORS, 1, rows * LANES), bf16),
@@ -470,11 +473,12 @@
             pltpu.VMEM((2, 2, rows, LANES), f32),
             pltpu.VMEM((CHUNKS, COLORS, rows, LANES), f32),
             pltpu.VMEM((GROUP, 1, vec_share), bf16),
+            pltpu.VMEM((3, 1, vec_share), f32),
             pltpu.VMEM((GROUP, 1, LANES), f32),
             pltpu.VMEM((8, LANES), f32),
             dma((SLOTS,)), dma((SLOTS,)), dma((2,)), dma((RING,)),
             dma((IN_FLIGHT,)), dma((2,)), dma((CHUNKS,)),
-            dma((COLORS, PIECES)), dma((COLORS, CHUNKS)), dma((COLORS, CHUNKS)), dma((7,)),
+            dma((COLORS, PIECES)), dma((COLORS, CHUNKS)), dma((COLORS, CHUNKS)), dma((7,)), dma,
             dma((COLORS,)), dma((7, COLORS, PIECES)), dma((COLORS,)), dma((COLORS,)),
         ],
         compiler_params=pltpu.CompilerParams(
@@ -483,7 +487,7 @@
 
 
 def store_kernel(*refs):
-    ins, outs, (vec_weights, sems) = refs[:8], refs[8:16], refs[16:]
+    ins, outs, (vec_wide, vec_weights, sems, vec_sem) = refs[:8], refs[8:16], refs[16:]
     land, vec_land = ins[6:]
     places = [(ins[index], outs[index]) for index in range(3, 6)]
     for index in range(3):
@@ -496,8 +500,10 @@
         copy.start()
     vec_rows = vec_land.shape[1]
     for owner in range(GROUP):
-        vec_weights[owner * vec_rows:(owner + 1) * vec_rows, :] = vec_land[owner]
-    outs[7][...] = vec_weights[...].astype(jnp.bfloat16)
+        vec_wide[owner * vec_rows:(owner + 1) * vec_rows, :] = vec_land[owner]
+    vec_weights[...] = vec_wide[...].astype(jnp.bfloat16)
+    copies.append(pltpu.make_async_copy(vec_weights, outs[7], vec_sem))
+    copies[-1].start()
     for copy in copies:
         copy.wait()
 
@@ -513,8 +519,8 @@
         out_shape=tuple(jax.ShapeDtypeStruct(result.shape, result.dtype) for result in results[:7]) + (
             jax.ShapeDtypeStruct((vec_rows, LANES), jnp.bfloat16),),
         in_specs=[vmem_spec] * 8,
-        out_specs=(hbm_spec,) * 7 + (vmem_spec,),
-        scratch_shapes=[pltpu.VMEM((vec_rows, LANES), jnp.float32), dma((3 + 3 * STATE_PARTS + GROUP,))],
+        out_specs=(hbm_spec,) * 8,
+        scratch_shapes=[pltpu.VMEM((vec_rows, LANES), jnp.float32), pltpu.VMEM((vec_rows, LANES), jnp.bfloat16), dma((3 + 3 * STATE_PARTS + GROUP,)), dma],
         compiler_params=pltpu.CompilerParams(vmem_limit_bytes=SCRATCH_BYTES),
     )(*[pltpu.with_memory_space_constraint(result, pltpu.VMEM) for result in results])
 

time: 405 us -> 404 us (level)
  no operation moved by 1% of the time
where the time goes in v11:
time: 404 us; the launch traced here: 402 us
  Pallas kernels  402 us (100%)
    pallas_call x1, Pallas kernels, step_call(): pl.pallas_call(functools.partial(step_kernel, rows, share, vec_share), na...  385 us
    pallas_call x1, Pallas kernels, store_call(): pl.pallas_call(store_kernel, name='store_results', out_shape=tuple((jax.S...  17.3 us

profile of v11, /device:TPU:0, one launch (start us, length us, event | category | flops | bytes accessed | tf_op | source)
XLA Modules:
  0.0 402.5 jit_solution(16540289968359277887)
XLA Ops:
  0.6 384.5 %adam_step.1 = (f32[9600,128]{1,0:T(8,128)S(1)}, f32[9600,128]{1,0:T(8,128)S(1)}, f32[9600,128]{1,0:T(8,128)S(1)}, f32[1,512]{1,0:T(1,128)S(1)}, f32[1,512]{1,0:...) custom-call(bf16[1,19660800]{1,0:T(2,128)(2,1)} %grad_ref.1, ...), custom_call_target="tpu_custom_call" | custom-call | tf_op jit(solution)/shard_map/adam_step/pallas_call | solution.py:460
  385.1 17.3 %store_results.1 = (f32[9600,128]{1,0:T(8,128)}, f32[9600,128]{1,0:T(8,128)}, f32[9600,128]{1,0:T(8,128)}, f32[1,512]{1,0:T(1,128)}, f32[1,512]{1,0:T(1,128)}, /...) custom-call(f32[9600,128]{1,0:T(8,128)S(1)} %get-tuple-element.24.refs_0_, ...), custom_call_target="tpu_custom_call" | custom-call | tf_op jit(solution)/shard_map/store_results/pallas_call | solution.py:516
